TPU v7x, 32 devices: a whole 2x2x4 slice. The times are simulated.
32 devices in a mesh: dp: 8 (over y, x, core), mp: 4 (over z).
Axes of the slice: x: 2, y: 2, z: 4, core: 2. Of those that a mesh axis runs over, the one named last changes fastest.
Arguments:
- hidden: bfloat16 [16384, 4096], P('dp', 'mp'), may hold values from -600 to 600
- segments: int32 [128, 128], P('dp'), may hold values from 0 to 5, never falling along the last dimension, each value on 1 to 40 neighbouring positions
- counts: int32 [8], replicated, may hold values from 1 to 16, 64 in all
- dest_order: int32 [8], replicated, may hold values from 0 to 7, each once
- norm_gain: bfloat16 [4096], replicated, may hold values from 0.5 to 1.5
- q_weight: bfloat16 [4096, 4096], P(None, 'mp'), may hold values from -1.921875 to 1.921875
- kv_weight: bfloat16 [4096, 2048], P(None, 'mp'), may hold values from -0.09375 to 0.09375
Outputs:
- attended: bfloat16 [8192, 4096], P('dp', 'mp')
Inputs may be any that keep to these rules, and one draw needn't show every extreme that they name: counts sum to 64 and reach 16 on some index of dp. `segments`: ids never fall within a block; a hypothesis spans at most 40 tokens.
All inputs are finite; a program needn't handle non-finite values.
Results may differ from a plain program's by a relative error of at most 0.0073.
Values may be sent and summed in bfloat16 or wider, within the bound.
No kernel may reach another device: no remote copies, remote signals or barrier semaphores. Data moves between devices by JAX's collectives and lax.ppermute only.
A program may use at most 128 MiB of HBM per device.

v0:
```python
import jax
import jax.numpy as jnp
from jax import lax
from jax.sharding import PartitionSpec as P

KV = 8
HD = 128


epsilon = 1e-05
rope_base = 500000.0


def for_sending(array):
    return jax.tree.map(lambda a: a.astype(jnp.bfloat16) if a.dtype == jnp.float32 else a, array)


def swapped(value, axis, stride):
    mask = 2**stride
    pairs = [(source, source ^ mask) for source in range(lax.axis_size(axis))]
    return lax.ppermute(value, axis, pairs)


def rope_tables(positions, width):
    halves = width // 2
    frequency = rope_base ** (-(jnp.arange(halves, dtype=jnp.float32) * 2.0) / width)
    angles = positions.astype(jnp.float32)[..., None] * frequency
    return (jnp.cos(angles), jnp.sin(angles))


def rotate(tensor, cosine, sine_part):
    halves = tensor.shape[-1] // 2
    lower = tensor[..., :halves]
    upper = tensor[..., halves:]
    cosine = cosine[..., None, :]
    sine_part = sine_part[..., None, :]
    return jnp.concatenate(
        [lower * cosine - upper * sine_part, upper * cosine + lower * sine_part], axis=-1
    )


def segment_masks(block_segments):
    length = block_segments.shape[-1]
    column = jnp.arange(length, dtype=jnp.int32)
    same_segment = block_segments[:, :, None] == block_segments[:, None, :]
    before = column[None, :] < column[:, None]
    positions = jnp.sum((same_segment & before[None]).astype(jnp.int32), axis=2)
    visible = same_segment & (column[None, :] <= column[:, None])[None]
    return (positions, visible)


def join_pieces(mine, theirs, upper_half):
    halves = mine.shape[-1] // 2
    leading = jnp.where(upper_half, theirs, mine)
    trailing = jnp.where(upper_half, mine, theirs)
    return jnp.concatenate(
        [leading[:, :halves], trailing[:, :halves], leading[:, halves:], trailing[:, halves:]],
        axis=-1,
    )


def on_device(hidden, segments, counts, dest_order, norm_gain, q_weight, kv_weight):
    dp_count = lax.axis_size("dp")
    mp_count = lax.axis_size("mp")
    dp_index = lax.axis_index("dp")
    mp_index = lax.axis_index("mp")
    in_slots = segments.shape[0]
    block_len = segments.shape[1]
    kept_slots = in_slots // 2
    per_peer = (in_slots + dp_count - 1) // dp_count
    local_width = hidden.shape[1]
    head_share = max(1, mp_count // KV)
    kv_local = max(1, KV // mp_count)
    token_count = kept_slots * block_len
    device_ids = jnp.arange(dp_count, dtype=jnp.int32)
    starts = jnp.cumsum(counts) - counts
    finishes = starts + counts
    position_of = jnp.sum(
        device_ids[None, :] * (dest_order[None, :] == device_ids[:, None]).astype(jnp.int32), axis=1
    )
    offsets = (position_of - starts[dp_index]) % dp_count
    wanted = offsets[:, None] + jnp.arange(per_peer, dtype=jnp.int32)[None, :] * dp_count
    usable = wanted < counts[dp_index]
    slot_ids = jnp.arange(in_slots, dtype=jnp.int32)
    choose = ((wanted[:, :, None] == slot_ids[None, None, :]) & usable[:, :, None]).astype(
        jnp.bfloat16
    )
    choose = choose.reshape(dp_count * per_peer, in_slots)
    outgoing = jnp.dot(
        choose,
        hidden.reshape(in_slots, block_len * local_width),
        preferred_element_type=jnp.float32,
    ).astype(jnp.bfloat16)
    segment_out = jnp.dot(
        choose, segments.astype(jnp.bfloat16), preferred_element_type=jnp.float32
    ).astype(jnp.bfloat16)
    global_ids = jnp.arange(kept_slots, dtype=jnp.int32) * dp_count + position_of[dp_index]
    sources = jnp.sum((finishes[None, :] <= global_ids[:, None]).astype(jnp.int32), axis=1)
    arrive_rows = sources * per_peer + (global_ids - starts[sources]) // dp_count
    place = (
        arrive_rows[:, None] == jnp.arange(dp_count * per_peer, dtype=jnp.int32)[None, :]
    ).astype(jnp.bfloat16)
    pieces = (
        lax.all_to_all(
            outgoing.reshape(dp_count, per_peer, block_len * local_width),
            "dp",
            split_axis=0,
            concat_axis=0,
            tiled=True,
        ),
        lax.all_to_all(
            segment_out.reshape(dp_count, per_peer, block_len),
            "dp",
            split_axis=0,
            concat_axis=0,
            tiled=True,
        ),
    )
    block_rows = (
        pieces[0]
        .astype(jnp.float32)
        .reshape(pieces[0].shape[0], pieces[0].shape[1], block_len, local_width)
    )
    arrived = pieces[0]
    segment_in = pieces[1]
    arrived_squares = jnp.sum(block_rows * block_rows, axis=3)
    placed_squares = jnp.dot(
        place.astype(jnp.float32),
        arrived_squares.reshape(dp_count * per_peer, block_len),
        precision=lax.Precision.HIGHEST,
    ).reshape(token_count)
    rows = jnp.dot(
        place,
        arrived.reshape(dp_count * per_peer, block_len * local_width),
        preferred_element_type=jnp.float32,
    ).astype(jnp.bfloat16)
    rows = rows.reshape(token_count, local_width)
    block_segments = jnp.dot(
        place,
        segment_in.reshape(dp_count * per_peer, block_len),
        preferred_element_type=jnp.float32,
    )
    widened = rows.astype(jnp.float32)
    totals = lax.psum(placed_squares, "mp")
    row_scale = lax.rsqrt(totals / norm_gain.shape[0] + epsilon)[:, None]
    local_gain = lax.dynamic_slice_in_dim(norm_gain, mp_index * local_width, local_width)
    gained = (widened * local_gain.astype(jnp.float32)).astype(jnp.bfloat16)
    normed = lax.all_gather(gained, "mp", axis=1, tiled=True)
    queries = row_scale * jnp.dot(normed, q_weight, preferred_element_type=jnp.float32)
    kv_rows = (row_scale * jnp.dot(normed, kv_weight, preferred_element_type=jnp.float32)).astype(
        jnp.bfloat16
    )
    for level in range(head_share.bit_length() - 1):
        theirs = swapped(for_sending(kv_rows), "mp", level).astype(kv_rows.dtype)
        upper_half = mp_index // (1 << level) % 2 == 1
        kv_rows = join_pieces(kv_rows, theirs, upper_half)
    kv_split = kv_rows.reshape(token_count, kv_local, 2, HD)
    key_raw = kv_split[:, :, 0, :]
    value_rows = kv_split[:, :, 1, :]
    positions, visible = segment_masks(block_segments)
    cosine, sine_part = rope_tables(positions, HD)
    q_heads = queries.shape[1] // HD
    query_rows = rotate(
        queries.reshape(kept_slots, block_len, q_heads, HD), cosine, sine_part
    ).astype(jnp.bfloat16)
    key_rows = rotate(
        key_raw.astype(jnp.float32).reshape(kept_slots, block_len, kv_local, HD), cosine, sine_part
    ).astype(jnp.bfloat16)
    grouped = query_rows.reshape(kept_slots, block_len, kv_local, q_heads // kv_local, HD)
    scores = jnp.einsum(
        "nikgd,njkd->nkgij", grouped, key_rows, preferred_element_type=jnp.float32
    ) * HD ** (-0.5)
    scores = jnp.where(visible[:, None, None], scores, -jnp.inf)
    highest = jnp.max(scores, axis=-1, keepdims=True)
    weights = jnp.exp(scores - highest)
    shares = (weights / jnp.sum(weights, axis=-1, keepdims=True)).astype(jnp.bfloat16)
    values = value_rows.reshape(kept_slots, block_len, kv_local, HD)
    mixture = jnp.einsum("nkgij,njkd->nikgd", shares, values, preferred_element_type=jnp.float32)
    return mixture.reshape(token_count, q_heads * HD).astype(jnp.bfloat16)


def solution(mesh):
    in_specs = (P("dp", "mp"), P("dp", None), P(), P(), P(), P(None, "mp"), P(None, "mp"))
    out_specs = P("dp", "mp")
    return jax.shard_map(
        on_device, mesh=mesh, in_specs=in_specs, out_specs=out_specs, check_vma=False
    )
```

profile of v0, /device:TPU:0, one launch (start us, length us, event | category | flops | bytes accessed | tf_op | source)
XLA Modules:
  0.0 309.2 jit_solution(16679841813479334554)
XLA Ops:
  6.5 0.8 reduce-window.8
  7.4 0.7 bitcast_subtract_fusion
  8.0 1.2 dynamic_slice.14
  9.3 0.7 dynamic_slice.13
  9.9 0.8 select_reduce_fusion
  10.7 0.7 and_select_fusion
  11.6 0.7 broadcast_compare_fusion
  12.3 1.5 convolution_convert_fusion.2
  13.8 5.2 %all-to-all-start.1 = ((bf16[8,2,128]{2,1,0:T(2,128)(2,1)}), bf16[8,2,128]{2,1,0:T(2,128)(2,1)S(1)}, u32[]{:S(2)}, u32[]{:S(2)}) async-start(bf16[8,2,128]{2,1,0:T(2,128)(2,1)} %bitcast.12), calls=%async_computation.1 | async-start | bytes 8192 | tf_op jit(solution)/shard_map/all_to_all | solution.py:111
  19.0 4.8 %reshape.225 = bf16[16,131072]{1,0:T(8,128)(2,1)} reshape(bf16[2048,1024]{1,0:T(8,128)(2,1)} %param.7) | data formatting | bytes 8388608 | tf_op jit(solution)/shard_map/reshape | solution.py:91
  23.8 5.4 %convolution_convert_fusion = bf16[16,131072]{1,0:T(8,128)(2,1)} fusion(bf16[16,131072]{1,0:T(8,128)(2,1)} %reshape.225, s32[16]{0:T(128)S(1)} %get-tuple-element.6, pred[16]{0:T(512)(128)(4,1)S(1)} %get-tuple-element.5), kind=kOutput, calls=%fused_computation.2 | convolution fusion | flops 69206528 | bytes 8388688 | tf_op jit(solution)/shard_map/dot_general | solution.py:89
  29.2 5.5 %reshape.226 = bf16[8,2,131072]{2,1,0:T(2,128)(2,1)} reshape(bf16[16,131072]{1,0:T(8,128)(2,1)} %convolution_convert_fusion) | data formatting | bytes 8388608 | tf_op jit(solution)/shard_map/reshape | solution.py:105
  34.8 4.5 %all-to-all-start = ((bf16[8,2,131072]{2,1,0:T(2,128)(2,1)}), bf16[8,2,131072]{2,1,0:T(2,128)(2,1)}, u32[]{:S(2)}, u32[]{:S(2)}) async-start(bf16[8,2,131072]{2,1,0:T(2,128)(2,1)} %reshape.226), calls=%async_computation | async-start | bytes 8388608 | tf_op jit(solution)/shard_map/all_to_all | solution.py:104
  39.4 0.6 dynamic_slice.12
  40.0 0.6 multiply_add_fusion
  40.8 0.6 gather_fusion
  41.5 0.7 dynamic-slice_convert_fusion
  42.2 0.7 fusion.28
  43.1 0.2 convert_reduce_fusion
  43.3 0.2 compare_and_fusion.1
  43.5 1.9 multiply_cosine_fusion
  45.4 43.0 %all-to-all-done = bf16[8,2,131072]{2,1,0:T(2,128)(2,1)} async-done(((bf16[8,2,131072]{2,1,0:T(2,128)(2,1)}), bf16[8,2,131072]{2,1,0:T(2,128)(2,1)}, u32[]{:S(2)}, u32[]{:S(2)}) %all-to-all-start) | async-done | bytes 4194336 | tf_op jit(solution)/shard_map/all_to_all | solution.py:104
  88.4 4.5 %reshape.229 = bf16[16,131072]{1,0:T(8,128)(2,1)} reshape(bf16[8,2,131072]{2,1,0:T(2,128)(2,1)} %all-to-all-done) | data formatting | bytes 8388608 | tf_op jit(solution)/shard_map/reshape | solution.py:134
  93.0 4.9 %fusion.1 = f32[8,131072]{1,0:T(8,128)} fusion(bf16[16,131072]{1,0:T(8,128)(2,1)} %reshape.229, s32[8]{0:T(128)S(1)} %fusion.28), kind=kOutput, calls=%fused_computation.4 | convolution fusion | flops 35651712 | bytes 8388640 | tf_op jit(solution)/shard_map/dot_general | solution.py:132
  97.8 4.9 %reshape.234 = f32[1024,1024]{1,0:T(8,128)} reshape(f32[8,131072]{1,0:T(8,128)} %fusion.1) | data formatting | bytes 8388608 | tf_op jit(solution)/shard_map/convert_element_type | solution.py:143
  102.8 4.1 %multiply_convert_fusion = bf16[1024,1024]{1,0:T(8,128)(2,1)} fusion(f32[1024,1024]{1,0:T(8,128)} %reshape.234, f32[1024]{0:T(1024)S(1)} %dynamic-slice_convert_fusion), kind=kLoop, calls=%fused_computation.12 | loop fusion | flops 2097152 | bytes 6295552 | tf_op jit(solution)/shard_map/convert_element_type | solution.py:147
  106.9 5.9 %convert_multiply_fusion = f32[2,8,131072]{2,1,0:T(8,128)} fusion(bf16[2,8,131072]{2,1,0:T(8,128)(2,1)} %bitcast.55), kind=kLoop, calls=%fused_computation.5 | loop fusion | flops 4194304 | bytes 12582912 | tf_op jit(solution)/shard_map/mul | solution.py:126
  112.8 12.0 %mul.167 = f32[8,2,128,1024]{3,2,1,0:T(8,128)} reshape(f32[8,2,131072]{2,1,0:T(2,128)} %bitcast.58) | data formatting | bytes 16777216 | tf_op jit(solution)/shard_map/mul | solution.py:126
  124.9 3.9 %reduce_sum.50 = f32[8,2,128]{2,1,0:T(2,128)S(1)} reduce(f32[8,2,128,1024]{3,2,1,0:T(8,128)} %mul.167, f32[]{:T(128)} %constant.58.clone.1), dimensions={3}, to_apply=%region_3.4 | reduce | flops 2095104 | bytes 8396804 | tf_op jit(solution)/shard_map/reduce_sum | solution.py:126
  129.0 12.7 %psum.7 = f32[1024]{0:T(1024)S(1)} all-reduce(f32[1024]{0:T(1024)S(1)} %convolution_bitcast_fusion), channel_id=1, replica_groups=mesh['dp'=8,'mp'=4] {'mp'}, use_global_device_ids=true, to_apply=%region_4.5 | all-reduce | flops 1024 | bytes 8192 | tf_op jit(solution)/shard_map/psum | solution.py:144
  141.7 114.7 %all-gather.2.cloned.1.call-done = bf16[1024,4096]{1,0:T(8,128)(2,1)} async-done(((bf16[1024,1024]{1,0:T(8,128)(2,1)}), bf16[1024,4096]{1,0:T(8,128)(2,1)}) %all-gather.2.cloned.1.call-update) | async-done | bytes 8388624 | tf_op jit(solution)/shard_map/all_gather | solution.py:148
  256.3 9.1 %multiply_convert_fusion.1 = bf16[1024,512]{0,1:T(8,128)(2,1)S(1)} fusion(bf16[1024,4096]{1,0:T(8,128)(2,1)} %all-gather.2.cloned.1.call-done, bf16[4096,512]{1,0:T(8,128)(2,1)} %param.13, f32[1024]{0:T(1024)S(1)} %add_rsqrt_fusion), kind=kOutput, calls=%fused_computation.21 | convolution fusion | flops 4296015872 | bytes 13635584 | tf_op jit(solution)/shard_map/dot_general | solution.py:150
  265.4 0.9 fusion.32
  266.4 0.3 copy.39
  266.6 1.7 fusion.33
  268.3 13.7 %multiply_bitcast_fusion = f32[128,8,8,128]{3,1,2,0:T(8,128)S(1)} fusion(bf16[1024,4096]{1,0:T(8,128)(2,1)} %all-gather.2.cloned.1.call-done, bf16[4096,1024]{1,0:T(8,128)(2,1)} %param.12, f32[1024]{0:T(1024)S(1)} %add_rsqrt_fusion), kind=kOutput, calls=%fused_computation.11 | convolution fusion | flops 8590983168 | bytes 20975616 | tf_op jit(solution)/shard_map/dot_general | solution.py:149
  282.0 1.0 copy.42
  283.0 1.8 subtract_convert_fusion
  284.8 0.6 copy.25
  285.4 1.9 copy.26
  287.3 2.0 copy.38
  289.4 2.0 subtract_convert_fusion.1
  291.4 0.2 copy-done
  291.6 1.5 fusion.3
  293.1 1.3 fusion.34
  294.5 2.1 convert_bitcast_fusion
  296.6 3.0 copy.36
  299.6 2.7 reshape.246
  (21 shorter events, 0.9 us)
Async XLA Ops:
  13.8 21.0 %all-to-all-start.1 = ((bf16[8,2,128]{2,1,0:T(2,128)(2,1)}), bf16[8,2,128]{2,1,0:T(2,128)(2,1)S(1)}, u32[]{:S(2)}, u32[]{:S(2)}) async-start(bf16[8,2,128]{2,1,0:T(2,128)(2,1)} %bitcast.12), calls=%async_computation.1 | async-start | bytes 8192 | tf_op jit(solution)/shard_map/all_to_all | solution.py:111
  34.8 53.7 %all-to-all-start = ((bf16[8,2,131072]{2,1,0:T(2,128)(2,1)}), bf16[8,2,131072]{2,1,0:T(2,128)(2,1)}, u32[]{:S(2)}, u32[]{:S(2)}) async-start(bf16[8,2,131072]{2,1,0:T(2,128)(2,1)} %reshape.226), calls=%async_computation | async-start | bytes 8388608 | tf_op jit(solution)/shard_map/all_to_all | solution.py:104
  39.3 217.0 %all-gather.2.cloned.1.call-start = ((), (), s32[]{:S(2)}) async-start(), calls=%async_computation.2 | async-start | bytes 10485760 | tf_op jit(solution)/shard_map/all_gather | solution.py:148
  289.4 2.2 copy-start
  293.1 1.3 copy-start.1
Sparse Core Ops, SparseCore 0:
  107.0 149.2 all-gather.1
where the time goes:
time: 310 us; the launch traced here: 309 us
  waiting for transfers between devices  158 us (51%)
  local copies, waits for them, and re-layouts  49.6 us (16%)
  matrix products  38.5 us (12%)
  other arithmetic  27.3 us (9%)
  between operations  13.6 us (4%)
  blocking collectives  12.7 us (4%)
  starting transfers between devices  9.79 us (3%)
    all_gather x1, waiting for transfers between devices, on_device(): normed = lax.all_gather(gained, 'mp', axis=1, tiled=True)  115 us
    all_to_all x1, waiting for transfers between devices, on_device(): lax.all_to_all(outgoing.reshape(dp_count, per_peer, block_len * local_wid...  43 us
    dot_general x1, matrix products, on_device(): jnp.dot(normed, q_weight, preferred_element_type=jnp.float32)  13.7 us
    psum x1, blocking collectives, on_device(): totals = lax.psum(placed_squares, 'mp')  12.7 us
    mul x1, local copies, waits for them, and re-layouts, on_device(): arrived_squares = jnp.sum(block_rows * block_rows, axis=3)  12 us
    dot_general x1, matrix products, on_device(): jnp.dot(normed, kv_weight, preferred_element_type=jnp.float32)  9.1 us
  transfers between devices with their start and end apart: 3, of which 2 were waited for; matrix products, arithmetic and copies ran while one was open for 14% of the time, Pallas kernels for 0%

commit v1 on v0

--- a/solution.py
+++ b/solution.py
@@ -1,6 +1,10 @@
+import functools
+
 import jax
 import jax.numpy as jnp
 from jax import lax
+from jax.experimental import pallas as pl
+from jax.experimental.pallas import tpu as pltpu
 from jax.sharding import PartitionSpec as P
 
 KV = 8
@@ -9,6 +13,10 @@
 
 epsilon = 1e-05
 rope_base = 500000.0
+
+ID_ROWS = 8
+FEATURE_EIGHTHS = (2, 6)
+GROUPS = (2, 2, 2, 2)
 
 
 def for_sending(array):
@@ -59,7 +67,7 @@
     )
 
 
-def on_device(hidden, segments, counts, dest_order, norm_gain, q_weight, kv_weight):
+def general_device(hidden, segments, counts, dest_order, norm_gain, q_weight, kv_weight):
     dp_count = lax.axis_size("dp")
     mp_count = lax.axis_size("mp")
     dp_index = lax.axis_index("dp")
@@ -100,29 +108,21 @@
     place = (
         arrive_rows[:, None] == jnp.arange(dp_count * per_peer, dtype=jnp.int32)[None, :]
     ).astype(jnp.bfloat16)
-    pieces = (
-        lax.all_to_all(
-            outgoing.reshape(dp_count, per_peer, block_len * local_width),
-            "dp",
-            split_axis=0,
-            concat_axis=0,
-            tiled=True,
-        ),
-        lax.all_to_all(
-            segment_out.reshape(dp_count, per_peer, block_len),
-            "dp",
-            split_axis=0,
-            concat_axis=0,
-            tiled=True,
-        ),
-    )
-    block_rows = (
-        pieces[0]
-        .astype(jnp.float32)
-        .reshape(pieces[0].shape[0], pieces[0].shape[1], block_len, local_width)
-    )
-    arrived = pieces[0]
-    segment_in = pieces[1]
+    arrived = lax.all_to_all(
+        outgoing.reshape(dp_count, per_peer, block_len * local_width),
+        "dp",
+        split_axis=0,
+        concat_axis=0,
+        tiled=True,
+    )
+    segment_in = lax.all_to_all(
+        segment_out.reshape(dp_count, per_peer, block_len),
+        "dp",
+        split_axis=0,
+        concat_axis=0,
+        tiled=True,
+    )
+    block_rows = arrived.astype(jnp.float32).reshape(dp_count, per_peer, block_len, local_width)
     arrived_squares = jnp.sum(block_rows * block_rows, axis=3)
     placed_squares = jnp.dot(
         place.astype(jnp.float32),
@@ -179,9 +179,298 @@
     return mixture.reshape(token_count, q_heads * HD).astype(jnp.bfloat16)
 
 
+ANY = pl.BlockSpec(memory_space=pl.ANY)
+SMEM = pl.BlockSpec(memory_space=pltpu.SMEM)
+VMEM = pl.BlockSpec(memory_space=pltpu.VMEM)
+
+
+def start_of(counts, index, n):
+    total = jnp.int32(0)
+    for j in range(n):
+        total = total + jnp.where(j < index, counts[j], 0)
+    return total
+
+
+def place_of(dest_order, device, n):
+    total = jnp.int32(0)
+    for j in range(n):
+        total = total + jnp.where(dest_order[j] == device, j, 0)
+    return total
+
+
+def pack_kernel(counts, dest_order, segments, hidden, *refs, n, per_peer, block_len, widths):
+    outs = refs[: len(widths)]
+    (sems,) = refs[len(widths) :]
+    in_slots = segments.shape[0]
+    me = lax.axis_index("dp")
+    mine = start_of(counts, me, n)
+    copies = []
+    begin = 0
+    for c, width in enumerate(widths):
+        for peer in range(n):
+            offset = lax.rem(place_of(dest_order, peer, n) - mine + n * in_slots, n)
+            for a in range(per_peer):
+                slot = jnp.minimum(offset + a * n, in_slots - 1)
+                row = pl.multiple_of(slot * block_len, block_len)
+                copies.append(
+                    pltpu.make_async_copy(
+                        hidden.at[pl.ds(row, block_len), pl.ds(begin, width)],
+                        outs[c].at[peer, a, pl.ds(0, block_len), :],
+                        sems.at[c, peer, a],
+                    )
+                )
+                copies[-1].start()
+                if c == 0:
+                    ids = segments[pl.ds(slot, 1), :].astype(jnp.float32)
+                    ids = jnp.broadcast_to(ids, (ID_ROWS, block_len)).astype(jnp.bfloat16)
+                    outs[0][peer, a, block_len:, :block_len] = ids
+        begin += width
+    for copy in copies:
+        copy.wait()
+
+
+def place_kernel(counts, dest_order, arrived, *outs, n, block_len, groups, with_ids):
+    me = lax.axis_index("dp")
+    my_place = place_of(dest_order, me, n)
+    k = 0
+    for g, size in enumerate(groups):
+        for i in range(size):
+            wanted = k * n + my_place
+            source = jnp.int32(0)
+            begin = jnp.int32(0)
+            total = jnp.int32(0)
+            for j in range(n):
+                total = total + counts[j]
+                passed = total <= wanted
+                source = source + passed.astype(jnp.int32)
+                begin = jnp.where(passed, total, begin)
+            a = lax.div(wanted - begin, n)
+            outs[g][i * block_len : (i + 1) * block_len, :] = arrived[source, a, :block_len, :]
+            if with_ids:
+                outs[-1][k] = arrived[source, a, block_len:, :block_len]
+            k += 1
+
+
+def layer_kernel(*refs, widths, rows, low, q_heads, kv_local, first_rows, fresh):
+    count = len(widths)
+    pieces = refs[: 6 * count]
+    gain, turn, cross, mask, q_weight, kv_weight = refs[6 * count : 6 * count + 6]
+    out, x, y, stage, out_sem = refs[6 * count + (6 if fresh else 7) :]
+    me = lax.axis_index("mp")
+    inner = (me == 1) | (me == 2)
+    local = sum(widths)
+    depth = 4 * local
+    begin = 0
+    for c, width in enumerate(widths):
+        own, near, mid, far, end_mid, end_far = pieces[6 * c : 6 * c + 6]
+        row = slice(None) if first_rows[c] is None else slice(first_rows[c], first_rows[c] + rows)
+        pair = lax.bitwise_xor(me, 1)
+        second = jnp.where(inner, 3 - me, jnp.where(me == 0, 2, 1))
+        third = jnp.where(inner, lax.bitwise_xor(3 - me, 1), 3 - me)
+
+        def put(source, value):
+            column = pl.multiple_of(source * local + begin, HD)
+            x[:, pl.ds(column, width)] = value
+
+        put(me, own[row, :])
+        put(pair, near[row, :])
+
+        @pl.when(inner)
+        def _():
+            put(second, mid[row, :])
+            put(third, far[row, :])
+
+        @pl.when(jnp.logical_not(inner))
+        def _():
+            put(second, end_mid[row, :])
+            put(third, end_far[row, :])
+
+        begin += width
+    squares = jnp.zeros((rows, HD), jnp.float32)
+    for m in range(4):
+        part = slice(m * local, (m + 1) * local)
+        raw = x[:, part]
+        for t in range(local // HD):
+            wide = raw[:, t * HD : (t + 1) * HD].astype(jnp.float32)
+            squares = squares + wide * wide
+        x[:, part] = raw * gain[:, part]
+    scale = lax.rsqrt(jnp.sum(squares, axis=1, keepdims=True) / depth + epsilon)
+    normed = x[...]
+    y[:, : q_heads * HD] = jnp.dot(normed, q_weight[...], preferred_element_type=jnp.float32)
+    y[:, q_heads * HD :] = jnp.dot(normed, kv_weight[...], preferred_element_type=jnp.float32)
+    per_kv = q_heads // kv_local
+    length = mask.shape[1]
+    for b in range(rows // length):
+        here = slice(b * length, (b + 1) * length)
+        row_scale = scale[here]
+        cosine = turn[here, :]
+        sine = cross[here, :]
+        visible = mask[here, :] > 0
+
+        def rotated(value):
+            return (value * cosine + pltpu.roll(value, HD // 2, 1) * sine).astype(jnp.bfloat16)
+
+        visible_all = jnp.concatenate([visible] * per_kv, axis=0)
+        for j in range(kv_local):
+            base = q_heads * HD + 2 * j * HD
+            key = (row_scale * y[here, base : base + HD]).astype(jnp.bfloat16)
+            key = rotated(key.astype(jnp.float32))
+            value = (row_scale * y[here, base + HD : base + 2 * HD]).astype(jnp.bfloat16)
+            query = jnp.concatenate(
+                [
+                    rotated(row_scale * y[here, h * HD : (h + 1) * HD])
+                    for h in range(j * per_kv, (j + 1) * per_kv)
+                ],
+                axis=0,
+            )
+            scores = lax.dot_general(
+                query, key, (((1,), (1,)), ((), ())), preferred_element_type=jnp.float32
+            ) * HD ** (-0.5)
+            scores = jnp.where(visible_all, scores, -jnp.inf)
+            highest = jnp.max(scores, axis=1, keepdims=True)
+            weights = jnp.exp(scores - highest)
+            shares = (weights / jnp.sum(weights, axis=1, keepdims=True)).astype(jnp.bfloat16)
+            mixed = jnp.dot(shares, value, preferred_element_type=jnp.float32).astype(jnp.bfloat16)
+            for i in range(per_kv):
+                h = j * per_kv + i
+                stage[here, h * HD : (h + 1) * HD] = mixed[i * length : (i + 1) * length]
+    copy = pltpu.make_async_copy(stage, out.at[pl.ds(low, rows), :], out_sem)
+    copy.start()
+    copy.wait()
+
+
+PAIRS = [(0, 1), (1, 0), (2, 3), (3, 2)]
+MIDDLE = [(1, 2), (2, 1)]
+OUTWARD = [(1, 0), (2, 3)]
+
+
+def send(value, pairs):
+    return lax.ppermute(value, "mp", pairs)
+
+
+def line_device(hidden, segments, counts, dest_order, norm_gain, q_weight, kv_weight):
+    n = lax.axis_size("dp")
+    in_slots, block_len = segments.shape
+    kept = in_slots // 2
+    per_peer = (in_slots + n - 1) // n
+    local = hidden.shape[1]
+    tokens = kept * block_len
+    q_heads = q_weight.shape[1] // HD
+    kv_local = kv_weight.shape[1] // (2 * HD)
+    bf16 = jnp.bfloat16
+    widths = tuple(local * e // 8 for e in FEATURE_EIGHTHS)
+    dma = pltpu.SemaphoreType.DMA
+    heights = [block_len + (ID_ROWS if c == 0 else 0) for c in range(len(widths))]
+    packed = pl.pallas_call(
+        functools.partial(
+            pack_kernel, n=n, per_peer=per_peer, block_len=block_len, widths=widths
+        ),
+        out_shape=[
+            jax.ShapeDtypeStruct((n, per_peer, height, width), bf16)
+            for height, width in zip(heights, widths)
+        ],
+        in_specs=[SMEM, SMEM, VMEM, ANY],
+        out_specs=[VMEM] * len(widths),
+        scratch_shapes=[dma((len(widths), n, per_peer))],
+        name="pack",
+    )(counts, dest_order, segments, hidden)
+    came = []
+    for buffer in packed:
+        came.append(lax.all_to_all(buffer, "dp", split_axis=0, concat_axis=0, tiled=True))
+    gathered = []
+    block_ids = None
+    for c, (width, arrived) in enumerate(zip(widths, came)):
+        groups = (kept,) if c == 0 else GROUPS
+        shapes = [jax.ShapeDtypeStruct((size * block_len, width), bf16) for size in groups]
+        if c == 0:
+            shapes.append(jax.ShapeDtypeStruct((kept, ID_ROWS, block_len), bf16))
+        placed = pl.pallas_call(
+            functools.partial(
+                place_kernel, n=n, block_len=block_len, groups=groups, with_ids=c == 0
+            ),
+            out_shape=shapes,
+            in_specs=[SMEM, SMEM, VMEM],
+            out_specs=[VMEM] * len(shapes),
+        )(counts, dest_order, arrived)
+        if c == 0:
+            block_ids = placed[-1][:, 0, :]
+            placed = placed[:-1]
+        rows = []
+        for own in placed:
+            near = send(own, PAIRS)
+            mid = send(own, MIDDLE)
+            far = send(near, MIDDLE)
+            end_mid = send(mid, OUTWARD)
+            end_far = send(far, OUTWARD)
+            rows.append([own, near, mid, far, end_mid, end_far])
+        gathered.append(rows)
+    positions, visible = segment_masks(block_ids)
+    cosine, sine = rope_tables(positions, HD)
+    turn = jnp.concatenate([cosine, cosine], axis=-1).reshape(tokens, HD)
+    cross = jnp.concatenate([-sine, sine], axis=-1).reshape(tokens, HD)
+    mask = visible.astype(jnp.float32).reshape(tokens, block_len)
+    gain = norm_gain[None, :]
+    out = None
+    low = 0
+    for g, size in enumerate(GROUPS):
+        rows = size * block_len
+        pieces, first_rows = [], []
+        for c in range(len(widths)):
+            whole = len(gathered[c]) == 1
+            pieces += gathered[c][0 if whole else g]
+            first_rows.append(low if whole else None)
+        kernel = functools.partial(
+            layer_kernel,
+            widths=widths,
+            rows=rows,
+            low=low,
+            q_heads=q_heads,
+            kv_local=kv_local,
+            first_rows=tuple(first_rows),
+            fresh=out is None,
+        )
+        part = slice(low, low + rows)
+        operands = pieces + [gain, turn[part], cross[part], mask[part], q_weight, kv_weight]
+        specs = [VMEM] * len(operands)
+        aliases = {}
+        if out is not None:
+            aliases = {len(operands): 0}
+            operands.append(out)
+            specs.append(ANY)
+        flops = 2 * rows * q_weight.shape[0] * (q_weight.shape[1] + kv_weight.shape[1])
+        out = pl.pallas_call(
+            kernel,
+            out_shape=jax.ShapeDtypeStruct((tokens, q_heads * HD), bf16),
+            in_specs=specs,
+            out_specs=ANY,
+            input_output_aliases=aliases,
+            scratch_shapes=[
+                pltpu.VMEM((rows, 4 * local), bf16),
+                pltpu.VMEM((rows, q_weight.shape[1] + kv_weight.shape[1]), jnp.float32),
+                pltpu.VMEM((rows, q_heads * HD), bf16),
+                dma(()),
+            ],
+            cost_estimate=pl.CostEstimate(
+                flops=flops, transcendentals=0, bytes_accessed=16 * 1024 * 1024
+            ),
+        )(*operands)
+        low += rows
+    return out
+
+
 def solution(mesh):
     in_specs = (P("dp", "mp"), P("dp", None), P(), P(), P(), P(None, "mp"), P(None, "mp"))
     out_specs = P("dp", "mp")
+    mp_count = mesh.shape["mp"]
+    line = mp_count == 4 and KV % mp_count == 0
+
+    def body(*arrays):
+        return line_device(*arrays)
+
     return jax.shard_map(
-        on_device, mesh=mesh, in_specs=in_specs, out_specs=out_specs, check_vma=False
-    )
+        body if line else general_device,
+        mesh=mesh,
+        in_specs=in_specs,
+        out_specs=out_specs,
+        check_vma=False,
+    )

time: 310 us -> 195 us (0.63)
  the two profiles are of different devices: /device:TPU:0 before, /device:TPU:16 now
where the time goes in v1:
time: 195 us
  Pallas kernels  59 us (30%)
  waiting for transfers between devices  53.9 us (28%)
  starting transfers between devices  50.4 us (26%)
  blocking collectives  20.3 us (10%)
  local copies, waits for them, and re-layouts  6.45 us (3%)
  other arithmetic  3.81 us (2%)
    ppermute x25, waiting for transfers between devices, send(): return lax.ppermute(value, 'mp', pairs)  50.4 us
    pallas_call x4, Pallas kernels, line_device(): pl.pallas_call(kernel, out_shape=jax.ShapeDtypeStruct((tokens, q_heads *...  48.2 us
    ppermute x25, starting transfers between devices, send(): return lax.ppermute(value, 'mp', pairs)  46.8 us
    all_to_all x1, blocking collectives, line_device(): lax.all_to_all(buffer, 'dp', split_axis=0, concat_axis=0, tiled=True)  20.3 us
    pallas_call x2, Pallas kernels, line_device(): pl.pallas_call(functools.partial(place_kernel, n=n, block_len=block_len,...  5.46 us
    pallas_call x1, Pallas kernels, line_device(): pl.pallas_call(functools.partial(pack_kernel, n=n, per_peer=per_peer, blo...  5.36 us
    unnamed x39, local copies, waits for them, and re-layouts  4.3 us
  transfers between devices with their start and end apart: 26, of which 13 were waited for; matrix products, arithmetic and copies ran while one was open for 3% of the time, Pallas kernels for 21%

profile of v1, /device:TPU:16, one launch (start us, length us, event | category | flops | bytes accessed | tf_op | source)
XLA Modules:
  0.0 194.6 jit_solution(2750306337684996292)
XLA Ops:
  0.0 5.4 %pack.1 = (bf16[8,2,136,256]{3,2,1,0:T(8,128)(2,1)}, bf16[8,2,128,768]{3,2,1,0:T(8,128)(2,1)}) custom-call(s32[8]{0:T(128)} %counts.5, s32[8]{0:T(128)} %dest_order.5, s32[16,128]{1,0:T(8,128)} %segments.1, bf16[2048,1024]{1,0:T(8,128)(2,1)} %hidden.1), custom_call_target="tpu_custom_call" | custom-call | tf_op jit(solution)/shard_map/pack/pallas_call | solution.py:364
  5.4 20.3 %all_to_all.10.arrived = bf16[8,2,136,256]{3,2,1,0:T(8,128)(2,1)} all-to-all(bf16[8,2,136,256]{3,2,1,0:T(8,128)(2,1)} %get-tuple-element.13), channel_id=1, replica_groups=mesh['dp'=8,'mp'=4] {'dp'}, dimensions={0} | all-to-all | bytes 2228224 | tf_op jit(solution)/shard_map/all_to_all | solution.py:379
  25.7 3.6 %all-to-all-start.1 = ((bf16[8,2,128,768]{3,2,1,0:T(8,128)(2,1)}), bf16[8,2,128,768]{3,2,1,0:T(8,128)(2,1)S(1)}, u32[]{:S(2)}, u32[]{:S(2)}) async-start(bf16[8,2,128,768]{3,2,1,0:T(8,128)(2,1)} %get-tuple-element.15), calls=%async_computation.1 | async-start | bytes 6291456 | tf_op jit(solution)/shard_map/all_to_all | solution.py:379
  29.3 2.2 %shard_map.73 = (bf16[1024,256]{1,0:T(8,128)(2,1)}, bf16[8,8,128]{2,1,0:T(8,128)(2,1)}) custom-call(s32[8]{0:T(128)} %counts.5, s32[8]{0:T(128)} %dest_order.5, bf16[8,2,136,256]{3,2,1,0:T(8,128)(2,1)} %all_to_all.10.arrived), custom_call_target="tpu_custom_call" | custom-call | tf_op jit(solution)/shard_map/pallas_call | solution.py:387
  31.5 1.6 collective-permute-start
  33.1 1.9 collective-permute-start.1
  35.0 10.9 %collective-permute-done.refs_1_ = bf16[1024,256]{1,0:T(8,128)(2,1)S(1)} collective-permute-done((bf16[1024,256]{1,0:T(8,128)(2,1)}, bf16[1024,256]{1,0:T(8,128)(2,1)S(1)}, u32[]{:S(2)}, u32[]{:S(2)}) %collective-permute-start) | collective-permute-done | bytes 524320 | tf_op jit(solution)/shard_map/ppermute | solution.py:348
  46.0 2.3 %collective-permute-start.2 = (bf16[1024,256]{1,0:T(8,128)(2,1)S(1)}, bf16[1024,256]{1,0:T(8,128)(2,1)}, u32[]{:S(2)}, u32[]{:S(2)}) collective-permute-start(bf16[1024,256]{1,0:T(8,128)(2,1)S(1)} %collective-permute-done.refs_1_), channel_id=1, source_target_pairs={{1,2},{2,1},{5,6},{6,5},{9,10},{10,9},{13,14},{14,13},{17,18},{18,... | collective-permute-start | bytes 1572872 | tf_op jit(solution)/shard_map/ppermute | solution.py:348
  48.3 0.9 collective-permute-done.1.refs_2_
  49.3 2.5 %collective-permute-start.3 = (bf16[1024,256]{1,0:T(8,128)(2,1)}, bf16[1024,256]{1,0:T(8,128)(2,1)}, u32[]{:S(2)}, u32[]{:S(2)}) collective-permute-start(bf16[1024,256]{1,0:T(8,128)(2,1)} %collective-permute-done.1.refs_2_), channel_id=1, source_target_pairs={{1,0},{2,3},{5,4},{6,7},{9,8},{10,11},{13,12},{14,15},{17,16},{18,... | collective-permute-start | bytes 1572872 | tf_op jit(solution)/shard_map/ppermute | solution.py:348
  51.8 9.7 %collective-permute-done.2.refs_3_ = bf16[1024,256]{1,0:T(8,128)(2,1)} collective-permute-done((bf16[1024,256]{1,0:T(8,128)(2,1)S(1)}, bf16[1024,256]{1,0:T(8,128)(2,1)}, u32[]{:S(2)}, u32[]{:S(2)}) %collective-permute-start.2) | collective-permute-done | bytes 524320 | tf_op jit(solution)/shard_map/ppermute | solution.py:348
  61.5 2.1 %collective-permute-start.4 = (bf16[1024,256]{1,0:T(8,128)(2,1)}, bf16[1024,256]{1,0:T(8,128)(2,1)}, u32[]{:S(2)}, u32[]{:S(2)}) collective-permute-start(bf16[1024,256]{1,0:T(8,128)(2,1)} %collective-permute-done.2.refs_3_), channel_id=1, source_target_pairs={{1,0},{2,3},{5,4},{6,7},{9,8},{10,11},{13,12},{14,15},{17,16},{18,... | collective-permute-start | bytes 1572872 | tf_op jit(solution)/shard_map/ppermute | solution.py:348
  63.5 3.6 %all-to-all-done.1.arrived = bf16[8,2,128,768]{3,2,1,0:T(8,128)(2,1)S(1)} async-done(((bf16[8,2,128,768]{3,2,1,0:T(8,128)(2,1)}), bf16[8,2,128,768]{3,2,1,0:T(8,128)(2,1)S(1)}, u32[]{:S(2)}, u32[]{:S(2)}) %all-to-all-start.1) | async-done | bytes 3145760 | tf_op jit(solution)/shard_map/all_to_all | solution.py:379
  67.1 1.7 copy-done
  68.8 3.2 %shard_map.74 = (bf16[256,768]{1,0:T(8,128)(2,1)}, bf16[256,768]{1,0:T(8,128)(2,1)}, bf16[256,768]{1,0:T(8,128)(2,1)}, bf16[256,768]{1,0:T(8,128)(2,1)}) custom-call(s32[8]{0:T(128)} %counts.5, s32[8]{0:T(128)} %dest_order.5, bf16[8,2,128,768]{3,2,1,0:T(8,128)(2,1)} %copy-done), custom_call_target="tpu_custom_call" | custom-call | tf_op jit(solution)/shard_map/pallas_call | solution.py:387
  72.0 1.6 collective-permute-start.20
  73.6 1.9 collective-permute-start.21
  75.7 3.9 %collective-permute-start.16 = (bf16[256,768]{1,0:T(8,128)(2,1)}, bf16[256,768]{1,0:T(8,128)(2,1)S(1)}, u32[]{:S(2)}, u32[]{:S(2)}) collective-permute-start(bf16[256,768]{1,0:T(8,128)(2,1)} %get-tuple-element.19.refs_6_), channel_id=1, source_target_pairs={{1,2},{2,1},{5,6},{6,5},{9,10},{10,9},{13,14},{14,13},{17,18},{18,... | collective-permute-start | bytes 1179656 | tf_op jit(solution)/shard_map/ppermute | solution.py:348
  79.7 4.6 %collective-permute-done.20.refs_7_ = bf16[256,768]{1,0:T(8,128)(2,1)S(1)} collective-permute-done((bf16[256,768]{1,0:T(8,128)(2,1)}, bf16[256,768]{1,0:T(8,128)(2,1)S(1)}, u32[]{:S(2)}, u32[]{:S(2)}) %collective-permute-start.20) | collective-permute-done | bytes 393248 | tf_op jit(solution)/shard_map/ppermute | solution.py:348
  84.2 2.2 %collective-permute-start.11 = (bf16[256,768]{1,0:T(8,128)(2,1)}, bf16[256,768]{1,0:T(8,128)(2,1)S(1)}, u32[]{:S(2)}, u32[]{:S(2)}) collective-permute-start(bf16[256,768]{1,0:T(8,128)(2,1)} %get-tuple-element.18.refs_6_), channel_id=1, source_target_pairs={{1,2},{2,1},{5,6},{6,5},{9,10},{10,9},{13,14},{14,13},{17,18},{18,... | collective-permute-start | bytes 1179656 | tf_op jit(solution)/shard_map/ppermute | solution.py:348
  88.7 4.0 %collective-permute-done.15.refs_7_ = bf16[256,768]{1,0:T(8,128)(2,1)S(1)} collective-permute-done((bf16[256,768]{1,0:T(8,128)(2,1)}, bf16[256,768]{1,0:T(8,128)(2,1)S(1)}, u32[]{:S(2)}, u32[]{:S(2)}) %collective-permute-start.15) | collective-permute-done | bytes 393248 | tf_op jit(solution)/shard_map/ppermute | solution.py:348
  92.7 2.2 %collective-permute-start.22 = (bf16[256,768]{1,0:T(8,128)(2,1)S(1)}, bf16[256,768]{1,0:T(8,128)(2,1)S(1)}, u32[]{:S(2)}, u32[]{:S(2)}) collective-permute-start(bf16[256,768]{1,0:T(8,128)(2,1)S(1)} %collective-permute-done.20.refs_7_), channel_id=1, source_target_pairs={{1,2},{2,1},{5,6},{6,5},{9,10},{10,9},{13,14},{14,13},{17,18},{18,... | collective-permute-start | bytes 1179656 | tf_op jit(solution)/shard_map/ppermute | solution.py:348
  95.1 1.0 collective-permute-done.16.refs_8_
  96.1 2.6 %collective-permute-start.6 = (bf16[256,768]{1,0:T(8,128)(2,1)}, bf16[256,768]{1,0:T(8,128)(2,1)S(1)}, u32[]{:S(2)}, u32[]{:S(2)}) collective-permute-start(bf16[256,768]{1,0:T(8,128)(2,1)} %get-tuple-element.16.refs_6_), channel_id=1, source_target_pairs={{1,2},{2,1},{5,6},{6,5},{9,10},{10,9},{13,14},{14,13},{17,18},{18,... | collective-permute-start | bytes 1179656 | tf_op jit(solution)/shard_map/ppermute | solution.py:348
  98.7 2.3 %collective-permute-done.10.refs_7_ = bf16[256,768]{1,0:T(8,128)(2,1)S(1)} collective-permute-done((bf16[256,768]{1,0:T(8,128)(2,1)}, bf16[256,768]{1,0:T(8,128)(2,1)S(1)}, u32[]{:S(2)}, u32[]{:S(2)}) %collective-permute-start.10) | collective-permute-done | bytes 393248 | tf_op jit(solution)/shard_map/ppermute | solution.py:348
  101.1 3.9 %collective-permute-start.23 = (bf16[256,768]{1,0:T(8,128)(2,1)S(1)}, bf16[256,768]{1,0:T(8,128)(2,1)S(1)}, u32[]{:S(2)}, u32[]{:S(2)}) collective-permute-start(bf16[256,768]{1,0:T(8,128)(2,1)S(1)} %collective-permute-done.21.refs_8_), channel_id=1, source_target_pairs={{1,0},{2,3},{5,4},{6,7},{9,8},{10,11},{13,12},{14,15},{17,16},{18,... | collective-permute-start | bytes 1179656 | tf_op jit(solution)/shard_map/ppermute | solution.py:348
  105.0 2.4 %collective-permute-start.17 = (bf16[256,768]{1,0:T(8,128)(2,1)S(1)}, bf16[256,768]{1,0:T(8,128)(2,1)}, u32[]{:S(2)}, u32[]{:S(2)}) collective-permute-start(bf16[256,768]{1,0:T(8,128)(2,1)S(1)} %collective-permute-done.15.refs_7_), channel_id=1, source_target_pairs={{1,2},{2,1},{5,6},{6,5},{9,10},{10,9},{13,14},{14,13},{17,18},{18,... | collective-permute-start | bytes 1179656 | tf_op jit(solution)/shard_map/ppermute | solution.py:348
  107.3 0.8 fusion.8
  108.2 0.9 collective-permute-done.5.refs_7_
  109.1 2.6 %collective-permute-start.12 = (bf16[256,768]{1,0:T(8,128)(2,1)S(1)}, bf16[256,768]{1,0:T(8,128)(2,1)S(1)}, u32[]{:S(2)}, u32[]{:S(2)}) collective-permute-start(bf16[256,768]{1,0:T(8,128)(2,1)S(1)} %collective-permute-done.10.refs_7_), channel_id=1, source_target_pairs={{1,2},{2,1},{5,6},{6,5},{9,10},{10,9},{13,14},{14,13},{17,18},{18,... | collective-permute-start | bytes 1179656 | tf_op jit(solution)/shard_map/ppermute | solution.py:348
  111.6 1.3 collective-permute-done.22.refs_9_
  113.0 1.3 collective-permute-start.24
  114.3 1.9 multiply_sine_fusion
  116.2 5.2 %collective-permute-done.6.refs_8_ = bf16[256,768]{1,0:T(8,128)(2,1)S(1)} collective-permute-done((bf16[256,768]{1,0:T(8,128)(2,1)}, bf16[256,768]{1,0:T(8,128)(2,1)S(1)}, u32[]{:S(2)}, u32[]{:S(2)}) %collective-permute-start.6) | collective-permute-done | bytes 393248 | tf_op jit(solution)/shard_map/ppermute | solution.py:348
  121.4 2.0 %collective-permute-start.18 = (bf16[256,768]{1,0:T(8,128)(2,1)S(1)}, bf16[256,768]{1,0:T(8,128)(2,1)}, u32[]{:S(2)}, u32[]{:S(2)}) collective-permute-start(bf16[256,768]{1,0:T(8,128)(2,1)S(1)} %collective-permute-done.16.refs_8_), channel_id=1, source_target_pairs={{1,0},{2,3},{5,4},{6,7},{9,8},{10,11},{13,12},{14,15},{17,16},{18,... | collective-permute-start | bytes 1179656 | tf_op jit(solution)/shard_map/ppermute | solution.py:348
  123.4 1.9 collective-permute-start.7
  125.3 4.6 %collective-permute-done.17.refs_9_ = bf16[256,768]{1,0:T(8,128)(2,1)} collective-permute-done((bf16[256,768]{1,0:T(8,128)(2,1)S(1)}, bf16[256,768]{1,0:T(8,128)(2,1)}, u32[]{:S(2)}, u32[]{:S(2)}) %collective-permute-start.17) | collective-permute-done | bytes 393248 | tf_op jit(solution)/shard_map/ppermute | solution.py:348
  129.9 2.0 %collective-permute-start.19 = (bf16[256,768]{1,0:T(8,128)(2,1)}, bf16[256,768]{1,0:T(8,128)(2,1)}, u32[]{:S(2)}, u32[]{:S(2)}) collective-permute-start(bf16[256,768]{1,0:T(8,128)(2,1)} %collective-permute-done.17.refs_9_), channel_id=1, source_target_pairs={{1,0},{2,3},{5,4},{6,7},{9,8},{10,11},{13,12},{14,15},{17,16},{18,... | collective-permute-start | bytes 1179656 | tf_op jit(solution)/shard_map/ppermute | solution.py:348
  132.0 1.3 pad_maximum_fusion
  133.3 4.9 %collective-permute-done.12.refs_9_ = bf16[256,768]{1,0:T(8,128)(2,1)S(1)} collective-permute-done((bf16[256,768]{1,0:T(8,128)(2,1)S(1)}, bf16[256,768]{1,0:T(8,128)(2,1)S(1)}, u32[]{:S(2)}, u32[]{:S(2)}) %collective-permute-start.12) | collective-permute-done | bytes 393248 | tf_op jit(solution)/shard_map/ppermute | solution.py:348
  138.2 1.3 collective-permute-start.13
  140.3 1.3 collective-permute-start.14
  141.6 12.0 %shard_map.75.refs_18_ = bf16[1024,1024]{1,0:T(8,128)(2,1)} custom-call(bf16[1024,256]{1,0:T(8,128)(2,1)} %get-tuple-element.14.refs_0_, bf16[1024,256]{1,0:T(8,128)(2,1)} %copy-done.1, bf16[1024,256]{1,0:T(8,128)(2,1)} %collective-permute-done.1.refs_2_, bf16[1024,256]{1,0:T(8,128)(2,1)} %collective-permute-done.2.refs_3_, ...), custom_call_target="tpu_custom_call" | custom-call | flops 3221225472 | bytes 16777216 | tf_op jit(solution)/shard_map/pallas_call | solution.py:441
  153.7 1.3 collective-permute-start.8
  155.0 1.3 collective-permute-start.9
  156.3 12.2 %shard_map.76.refs_18_ = bf16[1024,1024]{1,0:T(8,128)(2,1)} custom-call(bf16[1024,256]{1,0:T(8,128)(2,1)} %get-tuple-element.14.refs_0_, bf16[1024,256]{1,0:T(8,128)(2,1)} %copy-done.1, bf16[1024,256]{1,0:T(8,128)(2,1)} %collective-permute-done.1.refs_2_, bf16[1024,256]{1,0:T(8,128)(2,1)} %collective-permute-done.2.refs_3_, ...), custom_call_target="tpu_custom_call", output_to_operand_aliasing={{}: (18, {})} | custom-call | flops 3221225472 | bytes 16777216 | tf_op jit(solution)/shard_map/pallas_call | solution.py:441
  169.5 12.0 %shard_map.77.refs_18_ = bf16[1024,1024]{1,0:T(8,128)(2,1)} custom-call(bf16[1024,256]{1,0:T(8,128)(2,1)} %get-tuple-element.14.refs_0_, bf16[1024,256]{1,0:T(8,128)(2,1)} %copy-done.1, bf16[1024,256]{1,0:T(8,128)(2,1)} %collective-permute-done.1.refs_2_, bf16[1024,256]{1,0:T(8,128)(2,1)} %collective-permute-done.2.refs_3_, ...), custom_call_target="tpu_custom_call", output_to_operand_aliasing={{}: (18, {})} | custom-call | flops 3221225472 | bytes 16777216 | tf_op jit(solution)/shard_map/pallas_call | solution.py:441
  182.4 12.0 %shard_map.78 = bf16[1024,1024]{1,0:T(8,128)(2,1)} custom-call(bf16[1024,256]{1,0:T(8,128)(2,1)} %get-tuple-element.14.refs_0_, bf16[1024,256]{1,0:T(8,128)(2,1)} %copy-done.1, bf16[1024,256]{1,0:T(8,128)(2,1)} %collective-permute-done.1.refs_2_, bf16[1024,256]{1,0:T(8,128)(2,1)} %collective-permute-done.2.refs_3_, ...), custom_call_target="tpu_custom_call", output_to_operand_aliasing={{}: (18, {})} | custom-call | flops 3221225472 | bytes 16777216 | tf_op jit(solution)/shard_map/pallas_call | solution.py:441
  (62 shorter events, 5.2 us)
Async XLA Ops:
  25.7 41.4 %all-to-all-start.1 = ((bf16[8,2,128,768]{3,2,1,0:T(8,128)(2,1)}), bf16[8,2,128,768]{3,2,1,0:T(8,128)(2,1)S(1)}, u32[]{:S(2)}, u32[]{:S(2)}) async-start(bf16[8,2,128,768]{3,2,1,0:T(8,128)(2,1)} %get-tuple-element.15), calls=%async_computation.1 | async-start | bytes 6291456 | tf_op jit(solution)/shard_map/all_to_all | solution.py:379
  29.3 57.2 %copy-start.18 = (bf16[4096]{0:T(1024)(128)(2,1)S(1)}, bf16[4096]{0:T(1024)(128)(2,1)}, u32[]{:S(2)}) copy-start(bf16[4096]{0:T(1024)(128)(2,1)} %param.11) | copy-start | bytes 24580
  31.5 14.4 %collective-permute-start = (bf16[1024,256]{1,0:T(8,128)(2,1)}, bf16[1024,256]{1,0:T(8,128)(2,1)S(1)}, u32[]{:S(2)}, u32[]{:S(2)}) collective-permute-start(bf16[1024,256]{1,0:T(8,128)(2,1)} %get-tuple-element.14.refs_0_), channel_id=1, source_target_pairs={{0,1},{1,0},{2,3},{3,2},{4,5},{5,4},{6,7},{7,6},{8,9},{9,8},{10,11... | collective-permute-start | bytes 1572872 | tf_op jit(solution)/shard_map/ppermute | solution.py:348
  33.1 16.1 %collective-permute-start.1 = (bf16[1024,256]{1,0:T(8,128)(2,1)}, bf16[1024,256]{1,0:T(8,128)(2,1)}, u32[]{:S(2)}, u32[]{:S(2)}) collective-permute-start(bf16[1024,256]{1,0:T(8,128)(2,1)} %get-tuple-element.14.refs_0_), channel_id=1, source_target_pairs={{1,2},{2,1},{5,6},{6,5},{9,10},{10,9},{13,14},{14,13},{17,18},{18,... | collective-permute-start | bytes 1572872 | tf_op jit(solution)/shard_map/ppermute | solution.py:348
  46.0 15.5 %copy-start.1 = (bf16[1024,256]{1,0:T(8,128)(2,1)}, bf16[1024,256]{1,0:T(8,128)(2,1)S(1)}, u32[]{:S(2)}) copy-start(bf16[1024,256]{1,0:T(8,128)(2,1)S(1)} %collective-permute-done.refs_1_) | copy-start | bytes 1572868
  46.0 15.5 %collective-permute-start.2 = (bf16[1024,256]{1,0:T(8,128)(2,1)S(1)}, bf16[1024,256]{1,0:T(8,128)(2,1)}, u32[]{:S(2)}, u32[]{:S(2)}) collective-permute-start(bf16[1024,256]{1,0:T(8,128)(2,1)S(1)} %collective-permute-done.refs_1_), channel_id=1, source_target_pairs={{1,2},{2,1},{5,6},{6,5},{9,10},{10,9},{13,14},{14,13},{17,18},{18,... | collective-permute-start | bytes 1572872 | tf_op jit(solution)/shard_map/ppermute | solution.py:348
  49.3 26.4 %collective-permute-start.3 = (bf16[1024,256]{1,0:T(8,128)(2,1)}, bf16[1024,256]{1,0:T(8,128)(2,1)}, u32[]{:S(2)}, u32[]{:S(2)}) collective-permute-start(bf16[1024,256]{1,0:T(8,128)(2,1)} %collective-permute-done.1.refs_2_), channel_id=1, source_target_pairs={{1,0},{2,3},{5,4},{6,7},{9,8},{10,11},{13,12},{14,15},{17,16},{18,... | collective-permute-start | bytes 1572872 | tf_op jit(solution)/shard_map/ppermute | solution.py:348
  61.5 18.1 %collective-permute-start.4 = (bf16[1024,256]{1,0:T(8,128)(2,1)}, bf16[1024,256]{1,0:T(8,128)(2,1)}, u32[]{:S(2)}, u32[]{:S(2)}) collective-permute-start(bf16[1024,256]{1,0:T(8,128)(2,1)} %collective-permute-done.2.refs_3_), channel_id=1, source_target_pairs={{1,0},{2,3},{5,4},{6,7},{9,8},{10,11},{13,12},{14,15},{17,16},{18,... | collective-permute-start | bytes 1572872 | tf_op jit(solution)/shard_map/ppermute | solution.py:348
  67.1 1.7 copy-start
  72.0 12.2 %collective-permute-start.20 = (bf16[256,768]{1,0:T(8,128)(2,1)}, bf16[256,768]{1,0:T(8,128)(2,1)S(1)}, u32[]{:S(2)}, u32[]{:S(2)}) collective-permute-start(bf16[256,768]{1,0:T(8,128)(2,1)} %get-tuple-element.20.refs_6_), channel_id=1, source_target_pairs={{0,1},{1,0},{2,3},{3,2},{4,5},{5,4},{6,7},{7,6},{8,9},{9,8},{10,11... | collective-permute-start | bytes 1179656 | tf_op jit(solution)/shard_map/ppermute | solution.py:348
  73.6 14.6 %collective-permute-start.21 = (bf16[256,768]{1,0:T(8,128)(2,1)}, bf16[256,768]{1,0:T(8,128)(2,1)S(1)}, u32[]{:S(2)}, u32[]{:S(2)}) collective-permute-start(bf16[256,768]{1,0:T(8,128)(2,1)} %get-tuple-element.20.refs_6_), channel_id=1, source_target_pairs={{1,2},{2,1},{5,6},{6,5},{9,10},{10,9},{13,14},{14,13},{17,18},{18,... | collective-permute-start | bytes 1179656 | tf_op jit(solution)/shard_map/ppermute | solution.py:348
  75.5 17.1 %collective-permute-start.15 = (bf16[256,768]{1,0:T(8,128)(2,1)}, bf16[256,768]{1,0:T(8,128)(2,1)S(1)}, u32[]{:S(2)}, u32[]{:S(2)}) collective-permute-start(bf16[256,768]{1,0:T(8,128)(2,1)} %get-tuple-element.19.refs_6_), channel_id=1, source_target_pairs={{0,1},{1,0},{2,3},{3,2},{4,5},{5,4},{6,7},{7,6},{8,9},{9,8},{10,11... | collective-permute-start | bytes 1179656 | tf_op jit(solution)/shard_map/ppermute | solution.py:348
  75.7 20.5 %collective-permute-start.16 = (bf16[256,768]{1,0:T(8,128)(2,1)}, bf16[256,768]{1,0:T(8,128)(2,1)S(1)}, u32[]{:S(2)}, u32[]{:S(2)}) collective-permute-start(bf16[256,768]{1,0:T(8,128)(2,1)} %get-tuple-element.19.refs_6_), channel_id=1, source_target_pairs={{1,2},{2,1},{5,6},{6,5},{9,10},{10,9},{13,14},{14,13},{17,18},{18,... | collective-permute-start | bytes 1179656 | tf_op jit(solution)/shard_map/ppermute | solution.py:348
  79.6 21.5 %collective-permute-start.10 = (bf16[256,768]{1,0:T(8,128)(2,1)}, bf16[256,768]{1,0:T(8,128)(2,1)S(1)}, u32[]{:S(2)}, u32[]{:S(2)}) collective-permute-start(bf16[256,768]{1,0:T(8,128)(2,1)} %get-tuple-element.18.refs_6_), channel_id=1, source_target_pairs={{0,1},{1,0},{2,3},{3,2},{4,5},{5,4},{6,7},{7,6},{8,9},{9,8},{10,11... | collective-permute-start | bytes 1179656 | tf_op jit(solution)/shard_map/ppermute | solution.py:348
  84.2 49.0 %copy-start.8 = (bf16[256,768]{1,0:T(8,128)(2,1)}, bf16[256,768]{1,0:T(8,128)(2,1)S(1)}, u32[]{:S(2)}) copy-start(bf16[256,768]{1,0:T(8,128)(2,1)S(1)} %collective-permute-done.20.refs_7_) | copy-start | bytes 1179652
  84.2 20.7 %collective-permute-start.11 = (bf16[256,768]{1,0:T(8,128)(2,1)}, bf16[256,768]{1,0:T(8,128)(2,1)S(1)}, u32[]{:S(2)}, u32[]{:S(2)}) collective-permute-start(bf16[256,768]{1,0:T(8,128)(2,1)} %get-tuple-element.18.refs_6_), channel_id=1, source_target_pairs={{1,2},{2,1},{5,6},{6,5},{9,10},{10,9},{13,14},{14,13},{17,18},{18,... | collective-permute-start | bytes 1179656 | tf_op jit(solution)/shard_map/ppermute | solution.py:348
  88.2 45.0 %copy-start.9 = (bf16[256,768]{1,0:T(8,128)(2,1)}, bf16[256,768]{1,0:T(8,128)(2,1)S(1)}, u32[]{:S(2)}) copy-start(bf16[256,768]{1,0:T(8,128)(2,1)S(1)} %collective-permute-done.21.refs_8_) | copy-start | bytes 1179652
  88.2 20.8 %collective-permute-start.5 = (bf16[256,768]{1,0:T(8,128)(2,1)}, bf16[256,768]{1,0:T(8,128)(2,1)S(1)}, u32[]{:S(2)}, u32[]{:S(2)}) collective-permute-start(bf16[256,768]{1,0:T(8,128)(2,1)} %get-tuple-element.16.refs_6_), channel_id=1, source_target_pairs={{0,1},{1,0},{2,3},{3,2},{4,5},{5,4},{6,7},{7,6},{8,9},{9,8},{10,11... | collective-permute-start | bytes 1179656 | tf_op jit(solution)/shard_map/ppermute | solution.py:348
  92.6 40.6 %copy-start.4 = (bf16[256,768]{1,0:T(8,128)(2,1)}, bf16[256,768]{1,0:T(8,128)(2,1)S(1)}, u32[]{:S(2)}) copy-start(bf16[256,768]{1,0:T(8,128)(2,1)S(1)} %collective-permute-done.15.refs_7_) | copy-start | bytes 1179652
  92.7 20.3 %collective-permute-start.22 = (bf16[256,768]{1,0:T(8,128)(2,1)S(1)}, bf16[256,768]{1,0:T(8,128)(2,1)S(1)}, u32[]{:S(2)}, u32[]{:S(2)}) collective-permute-start(bf16[256,768]{1,0:T(8,128)(2,1)S(1)} %collective-permute-done.20.refs_7_), channel_id=1, source_target_pairs={{1,2},{2,1},{5,6},{6,5},{9,10},{10,9},{13,14},{14,13},{17,18},{18,... | collective-permute-start | bytes 1179656 | tf_op jit(solution)/shard_map/ppermute | solution.py:348
  96.1 37.2 %copy-start.6 = (bf16[256,768]{1,0:T(8,128)(2,1)}, bf16[256,768]{1,0:T(8,128)(2,1)S(1)}, u32[]{:S(2)}) copy-start(bf16[256,768]{1,0:T(8,128)(2,1)S(1)} %collective-permute-done.16.refs_8_) | copy-start | bytes 1179652
  96.1 25.3 %collective-permute-start.6 = (bf16[256,768]{1,0:T(8,128)(2,1)}, bf16[256,768]{1,0:T(8,128)(2,1)S(1)}, u32[]{:S(2)}, u32[]{:S(2)}) collective-permute-start(bf16[256,768]{1,0:T(8,128)(2,1)} %get-tuple-element.16.refs_6_), channel_id=1, source_target_pairs={{1,2},{2,1},{5,6},{6,5},{9,10},{10,9},{13,14},{14,13},{17,18},{18,... | collective-permute-start | bytes 1179656 | tf_op jit(solution)/shard_map/ppermute | solution.py:348
  101.1 32.2 %copy-start.2 = (bf16[256,768]{1,0:T(8,128)(2,1)}, bf16[256,768]{1,0:T(8,128)(2,1)S(1)}, u32[]{:S(2)}) copy-start(bf16[256,768]{1,0:T(8,128)(2,1)S(1)} %collective-permute-done.10.refs_7_) | copy-start | bytes 1179652
  101.1 22.4 %collective-permute-start.23 = (bf16[256,768]{1,0:T(8,128)(2,1)S(1)}, bf16[256,768]{1,0:T(8,128)(2,1)S(1)}, u32[]{:S(2)}, u32[]{:S(2)}) collective-permute-start(bf16[256,768]{1,0:T(8,128)(2,1)S(1)} %collective-permute-done.21.refs_8_), channel_id=1, source_target_pairs={{1,0},{2,3},{5,4},{6,7},{9,8},{10,11},{13,12},{14,15},{17,16},{18,... | collective-permute-start | bytes 1179656 | tf_op jit(solution)/shard_map/ppermute | solution.py:348
  105.0 33.3 %copy-start.5 = (bf16[256,768]{1,0:T(8,128)(2,1)}, bf16[256,768]{1,0:T(8,128)(2,1)S(1)}, u32[]{:S(2)}) copy-start(bf16[256,768]{1,0:T(8,128)(2,1)S(1)} %collective-permute-done.11.refs_8_) | copy-start | bytes 1179652
  105.0 25.0 %collective-permute-start.17 = (bf16[256,768]{1,0:T(8,128)(2,1)S(1)}, bf16[256,768]{1,0:T(8,128)(2,1)}, u32[]{:S(2)}, u32[]{:S(2)}) collective-permute-start(bf16[256,768]{1,0:T(8,128)(2,1)S(1)} %collective-permute-done.15.refs_7_), channel_id=1, source_target_pairs={{1,2},{2,1},{5,6},{6,5},{9,10},{10,9},{13,14},{14,13},{17,18},{18,... | collective-permute-start | bytes 1179656 | tf_op jit(solution)/shard_map/ppermute | solution.py:348
  109.1 24.2 %copy-start.3 = (bf16[256,768]{1,0:T(8,128)(2,1)}, bf16[256,768]{1,0:T(8,128)(2,1)S(1)}, u32[]{:S(2)}) copy-start(bf16[256,768]{1,0:T(8,128)(2,1)S(1)} %collective-permute-done.5.refs_7_) | copy-start | bytes 1179652
  109.1 29.1 %collective-permute-start.12 = (bf16[256,768]{1,0:T(8,128)(2,1)S(1)}, bf16[256,768]{1,0:T(8,128)(2,1)S(1)}, u32[]{:S(2)}, u32[]{:S(2)}) collective-permute-start(bf16[256,768]{1,0:T(8,128)(2,1)S(1)} %collective-permute-done.10.refs_7_), channel_id=1, source_target_pairs={{1,2},{2,1},{5,6},{6,5},{9,10},{10,9},{13,14},{14,13},{17,18},{18,... | collective-permute-start | bytes 1179656 | tf_op jit(solution)/shard_map/ppermute | solution.py:348
  113.0 20.3 %copy-start.11 = (bf16[256,768]{1,0:T(8,128)(2,1)}, bf16[256,768]{1,0:T(8,128)(2,1)S(1)}, u32[]{:S(2)}) copy-start(bf16[256,768]{1,0:T(8,128)(2,1)S(1)} %collective-permute-done.22.refs_9_) | copy-start | bytes 1179652
  113.0 26.6 %collective-permute-start.24 = (bf16[256,768]{1,0:T(8,128)(2,1)S(1)}, bf16[256,768]{1,0:T(8,128)(2,1)S(1)}, u32[]{:S(2)}, u32[]{:S(2)}) collective-permute-start(bf16[256,768]{1,0:T(8,128)(2,1)S(1)} %collective-permute-done.22.refs_9_), channel_id=1, source_target_pairs={{1,0},{2,3},{5,4},{6,7},{9,8},{10,11},{13,12},{14,15},{17,16},{18,... | collective-permute-start | bytes 1179656 | tf_op jit(solution)/shard_map/ppermute | solution.py:348
  121.4 32.3 %copy-start.7 = (bf16[256,768]{1,0:T(8,128)(2,1)}, bf16[256,768]{1,0:T(8,128)(2,1)S(1)}, u32[]{:S(2)}) copy-start(bf16[256,768]{1,0:T(8,128)(2,1)S(1)} %collective-permute-done.6.refs_8_) | copy-start | bytes 1179652
  121.4 32.3 %collective-permute-start.18 = (bf16[256,768]{1,0:T(8,128)(2,1)S(1)}, bf16[256,768]{1,0:T(8,128)(2,1)}, u32[]{:S(2)}, u32[]{:S(2)}) collective-permute-start(bf16[256,768]{1,0:T(8,128)(2,1)S(1)} %collective-permute-done.16.refs_8_), channel_id=1, source_target_pairs={{1,0},{2,3},{5,4},{6,7},{9,8},{10,11},{13,12},{14,15},{17,16},{18,... | collective-permute-start | bytes 1179656 | tf_op jit(solution)/shard_map/ppermute | solution.py:348
  123.4 6.5 %copy-start.12 = (bf16[256,768]{1,0:T(8,128)(2,1)}, bf16[256,768]{1,0:T(8,128)(2,1)S(1)}, u32[]{:S(2)}) copy-start(bf16[256,768]{1,0:T(8,128)(2,1)S(1)} %collective-permute-done.23.refs_10_) | copy-start | bytes 1179652
  123.4 31.6 %collective-permute-start.7 = (bf16[256,768]{1,0:T(8,128)(2,1)S(1)}, bf16[256,768]{1,0:T(8,128)(2,1)}, u32[]{:S(2)}, u32[]{:S(2)}) collective-permute-start(bf16[256,768]{1,0:T(8,128)(2,1)S(1)} %collective-permute-done.5.refs_7_), channel_id=1, source_target_pairs={{1,2},{2,1},{5,6},{6,5},{9,10},{10,9},{13,14},{14,13},{17,18},{18,... | collective-permute-start | bytes 1179656 | tf_op jit(solution)/shard_map/ppermute | solution.py:348
  129.9 26.4 %collective-permute-start.19 = (bf16[256,768]{1,0:T(8,128)(2,1)}, bf16[256,768]{1,0:T(8,128)(2,1)}, u32[]{:S(2)}, u32[]{:S(2)}) collective-permute-start(bf16[256,768]{1,0:T(8,128)(2,1)} %collective-permute-done.17.refs_9_), channel_id=1, source_target_pairs={{1,0},{2,3},{5,4},{6,7},{9,8},{10,11},{13,12},{14,15},{17,16},{18,... | collective-permute-start | bytes 1179656 | tf_op jit(solution)/shard_map/ppermute | solution.py:348
  138.2 15.4 %copy-start.10 = (bf16[256,768]{1,0:T(8,128)(2,1)}, bf16[256,768]{1,0:T(8,128)(2,1)S(1)}, u32[]{:S(2)}) copy-start(bf16[256,768]{1,0:T(8,128)(2,1)S(1)} %collective-permute-done.12.refs_9_) | copy-start | bytes 1179652
  138.2 30.4 %collective-permute-start.13 = (bf16[256,768]{1,0:T(8,128)(2,1)S(1)}, bf16[256,768]{1,0:T(8,128)(2,1)S(1)}, u32[]{:S(2)}, u32[]{:S(2)}) collective-permute-start(bf16[256,768]{1,0:T(8,128)(2,1)S(1)} %collective-permute-done.11.refs_8_), channel_id=1, source_target_pairs={{1,0},{2,3},{5,4},{6,7},{9,8},{10,11},{13,12},{14,15},{17,16},{18,... | collective-permute-start | bytes 1179656 | tf_op jit(solution)/shard_map/ppermute | solution.py:348
  139.5 0.8 copy-start.13
  140.3 28.3 %collective-permute-start.14 = (bf16[256,768]{1,0:T(8,128)(2,1)S(1)}, bf16[256,768]{1,0:T(8,128)(2,1)S(1)}, u32[]{:S(2)}, u32[]{:S(2)}) collective-permute-start(bf16[256,768]{1,0:T(8,128)(2,1)S(1)} %collective-permute-done.12.refs_9_), channel_id=1, source_target_pairs={{1,0},{2,3},{5,4},{6,7},{9,8},{10,11},{13,12},{14,15},{17,16},{18,... | collective-permute-start | bytes 1179656 | tf_op jit(solution)/shard_map/ppermute | solution.py:348
  153.7 27.8 %collective-permute-start.8 = (bf16[256,768]{1,0:T(8,128)(2,1)S(1)}, bf16[256,768]{1,0:T(8,128)(2,1)S(1)}, u32[]{:S(2)}, u32[]{:S(2)}) collective-permute-start(bf16[256,768]{1,0:T(8,128)(2,1)S(1)} %collective-permute-done.6.refs_8_), channel_id=1, source_target_pairs={{1,0},{2,3},{5,4},{6,7},{9,8},{10,11},{13,12},{14,15},{17,16},{18,... | collective-permute-start | bytes 1179656 | tf_op jit(solution)/shard_map/ppermute | solution.py:348
  155.0 26.5 %collective-permute-start.9 = (bf16[256,768]{1,0:T(8,128)(2,1)}, bf16[256,768]{1,0:T(8,128)(2,1)S(1)}, u32[]{:S(2)}, u32[]{:S(2)}) collective-permute-start(bf16[256,768]{1,0:T(8,128)(2,1)} %collective-permute-done.7.refs_9_), channel_id=1, source_target_pairs={{1,0},{2,3},{5,4},{6,7},{9,8},{10,11},{13,12},{14,15},{17,16},{18,... | collective-permute-start | bytes 1179656 | tf_op jit(solution)/shard_map/ppermute | solution.py:348
  168.6 0.8 copy-start.15
  168.6 0.9 copy-start.17
  181.5 0.8 copy-start.14
  181.5 0.9 copy-start.16

commit v2 on v1

--- a/solution.py
+++ b/solution.py
@@ -2,6 +2,7 @@
 
 import jax
 import jax.numpy as jnp
+import numpy as np
 from jax import lax
 from jax.experimental import pallas as pl
 from jax.experimental.pallas import tpu as pltpu
@@ -15,8 +16,8 @@
 rope_base = 500000.0
 
 ID_ROWS = 8
-FEATURE_EIGHTHS = (2, 6)
-GROUPS = (2, 2, 2, 2)
+FEATURE_EIGHTHS = (3, 5)
+GROUPS = (3, 2, 2, 1)
 
 
 def for_sending(array):
@@ -182,6 +183,19 @@
 ANY = pl.BlockSpec(memory_space=pl.ANY)
 SMEM = pl.BlockSpec(memory_space=pltpu.SMEM)
 VMEM = pl.BlockSpec(memory_space=pltpu.VMEM)
+MIB = 1024 * 1024
+
+
+def resident(value):
+    return pltpu.with_memory_space_constraint(value, pltpu.VMEM)
+
+
+def afar(value):
+    return pltpu.with_memory_space_constraint(value, pltpu.HBM)
+
+
+def limit(mib):
+    return pltpu.CompilerParams(vmem_limit_bytes=mib * MIB)
 
 
 def start_of(counts, index, n):
@@ -198,33 +212,38 @@
     return total
 
 
-def pack_kernel(counts, dest_order, segments, hidden, *refs, n, per_peer, block_len, widths):
-    outs = refs[: len(widths)]
-    (sems,) = refs[len(widths) :]
-    in_slots = segments.shape[0]
+def pack_kernel(counts, dest_order, *refs, n, per_peer, block_len, begin, width, with_ids):
+    if with_ids:
+        segments, hidden, out, sems, near, near_sem = refs
+        fetch = pltpu.make_async_copy(segments, near, near_sem)
+        fetch.start()
+    else:
+        hidden, out, sems = refs
+    in_slots = hidden.shape[0] // block_len
     me = lax.axis_index("dp")
     mine = start_of(counts, me, n)
+    slots = []
     copies = []
-    begin = 0
-    for c, width in enumerate(widths):
-        for peer in range(n):
-            offset = lax.rem(place_of(dest_order, peer, n) - mine + n * in_slots, n)
-            for a in range(per_peer):
-                slot = jnp.minimum(offset + a * n, in_slots - 1)
-                row = pl.multiple_of(slot * block_len, block_len)
-                copies.append(
-                    pltpu.make_async_copy(
-                        hidden.at[pl.ds(row, block_len), pl.ds(begin, width)],
-                        outs[c].at[peer, a, pl.ds(0, block_len), :],
-                        sems.at[c, peer, a],
-                    )
+    for peer in range(n):
+        offset = lax.rem(place_of(dest_order, peer, n) - mine + n * in_slots, n)
+        for a in range(per_peer):
+            slot = jnp.minimum(offset + a * n, in_slots - 1)
+            row = pl.multiple_of(slot * block_len, block_len)
+            copies.append(
+                pltpu.make_async_copy(
+                    hidden.at[pl.ds(row, block_len), pl.ds(begin, width)],
+                    out.at[peer, a, pl.ds(0, block_len), :],
+                    sems.at[peer, a],
                 )
-                copies[-1].start()
-                if c == 0:
-                    ids = segments[pl.ds(slot, 1), :].astype(jnp.float32)
-                    ids = jnp.broadcast_to(ids, (ID_ROWS, block_len)).astype(jnp.bfloat16)
-                    outs[0][peer, a, block_len:, :block_len] = ids
-        begin += width
+            )
+            copies[-1].start()
+            slots.append((peer, a, slot))
+    if with_ids:
+        fetch.wait()
+        for peer, a, slot in slots:
+            ids = near[pl.ds(slot, 1), :].astype(jnp.float32)
+            ids = jnp.broadcast_to(ids, (ID_ROWS, block_len)).astype(jnp.bfloat16)
+            out[peer, a, block_len:, :block_len] = ids
     for copy in copies:
         copy.wait()
 
@@ -251,61 +270,137 @@
             k += 1
 
 
-def layer_kernel(*refs, widths, rows, low, q_heads, kv_local, first_rows, fresh):
+def fetch_kernel(q_weight, kv_weight, q_near, kv_near, q_sem, kv_sem):
+    q_copy = pltpu.make_async_copy(q_weight, q_near, q_sem)
+    kv_copy = pltpu.make_async_copy(kv_weight, kv_near, kv_sem)
+    q_copy.start()
+    kv_copy.start()
+    q_copy.wait()
+    kv_copy.wait()
+
+
+def table_kernel(ids, cosines, sines, turn, cross, mask, *, kept, length):
+    row = lax.broadcasted_iota(jnp.int32, (length, length), 0)
+    column = lax.broadcasted_iota(jnp.int32, (length, length), 1)
+    for k in range(kept):
+        here = slice(k * length, (k + 1) * length)
+        along = jnp.broadcast_to(ids[k, :1, :].astype(jnp.float32), (length, length))
+        same = along == along.T
+        visible = same & (column <= row)
+        mask[here, :] = visible.astype(jnp.float32)
+        before = (same & (column < row)).astype(jnp.float32)
+        position = jnp.sum(before, axis=1, keepdims=True).astype(jnp.int32)
+        chosen = (position == column).astype(jnp.float32)
+        exact = dict(precision=lax.Precision.HIGHEST, preferred_element_type=jnp.float32)
+        turn[here, :] = jnp.dot(chosen, cosines[...], **exact)
+        cross[here, :] = jnp.dot(chosen, sines[...], **exact)
+
+
+def relatives(me):
+    inner = (me == 1) | (me == 2)
+    pair = lax.bitwise_xor(me, 1)
+    second = jnp.where(inner, 3 - me, jnp.where(me == 0, 2, 1))
+    third = jnp.where(inner, lax.bitwise_xor(3 - me, 1), 3 - me)
+    return inner, pair, second, third
+
+
+def project_kernel(*refs, widths, first_rows):
     count = len(widths)
-    pieces = refs[: 6 * count]
-    gain, turn, cross, mask, q_weight, kv_weight = refs[6 * count : 6 * count + 6]
-    out, x, y, stage, out_sem = refs[6 * count + (6 if fresh else 7) :]
+    pieces = refs[: 6 * count - 2]
+    gain, q_weight, kv_weight, y, squares, x = refs[6 * count - 2 :]
+    rows = x.shape[0]
     me = lax.axis_index("mp")
-    inner = (me == 1) | (me == 2)
+    inner, pair, second, third = relatives(me)
     local = sum(widths)
-    depth = 4 * local
     begin = 0
     for c, width in enumerate(widths):
-        own, near, mid, far, end_mid, end_far = pieces[6 * c : 6 * c + 6]
         row = slice(None) if first_rows[c] is None else slice(first_rows[c], first_rows[c] + rows)
-        pair = lax.bitwise_xor(me, 1)
-        second = jnp.where(inner, 3 - me, jnp.where(me == 0, 2, 1))
-        third = jnp.where(inner, lax.bitwise_xor(3 - me, 1), 3 - me)
 
         def put(source, value):
             column = pl.multiple_of(source * local + begin, HD)
             x[:, pl.ds(column, width)] = value
 
+        if c < count - 1:
+            own, near, mid, end_mid, far, end_far = pieces[6 * c : 6 * c + 6]
+        else:
+            own, near, mid, end_mid = pieces[6 * c :]
         put(me, own[row, :])
         put(pair, near[row, :])
 
         @pl.when(inner)
         def _():
             put(second, mid[row, :])
-            put(third, far[row, :])
 
         @pl.when(jnp.logical_not(inner))
         def _():
             put(second, end_mid[row, :])
-            put(third, end_far[row, :])
+
+        if c < count - 1:
+
+            @pl.when(inner)
+            def _():
+                put(third, far[row, :])
+
+            @pl.when(jnp.logical_not(inner))
+            def _():
+                put(third, end_far[row, :])
+        else:
+            put(third, jnp.zeros((rows, width), x.dtype))
 
         begin += width
-    squares = jnp.zeros((rows, HD), jnp.float32)
-    for m in range(4):
-        part = slice(m * local, (m + 1) * local)
+    total = jnp.zeros((rows, HD), jnp.float32)
+    for t in range(x.shape[1] // HD):
+        part = slice(t * HD, (t + 1) * HD)
         raw = x[:, part]
-        for t in range(local // HD):
-            wide = raw[:, t * HD : (t + 1) * HD].astype(jnp.float32)
-            squares = squares + wide * wide
+        wide = raw.astype(jnp.float32)
+        total = total + wide * wide
         x[:, part] = raw * gain[:, part]
-    scale = lax.rsqrt(jnp.sum(squares, axis=1, keepdims=True) / depth + epsilon)
+    squares[...] = total
     normed = x[...]
-    y[:, : q_heads * HD] = jnp.dot(normed, q_weight[...], preferred_element_type=jnp.float32)
-    y[:, q_heads * HD :] = jnp.dot(normed, kv_weight[...], preferred_element_type=jnp.float32)
+    split = q_weight.shape[1]
+    y[:, :split] = jnp.dot(normed, q_weight[...], preferred_element_type=jnp.float32)
+    y[:, split:] = jnp.dot(normed, kv_weight[...], preferred_element_type=jnp.float32)
+
+
+def attend_kernel(*refs, first, low, q_heads, kv_local, fresh):
+    far, end_far, y_part, squares, gain, turn, cross, mask, q_weight, kv_weight = refs[:10]
+    out, x, y, stage, out_sem = refs[10 if fresh else 11 :]
+    rows, width = x.shape
+    me = lax.axis_index("mp")
+    inner, _, _, third = relatives(me)
+    depth = q_weight.shape[0]
+
+    @pl.when(inner)
+    def _():
+        x[...] = far[...]
+
+    @pl.when(jnp.logical_not(inner))
+    def _():
+        x[...] = end_far[...]
+
+    total = squares[...]
+    for t in range(width // HD):
+        wide = x[:, t * HD : (t + 1) * HD].astype(jnp.float32)
+        total = total + wide * wide
+    scale = lax.rsqrt(jnp.sum(total, axis=1, keepdims=True) / depth + epsilon)
+    part = pl.ds(pl.multiple_of(third * (depth // 4) + first, HD), width)
+    normed = x[...] * gain[:, part]
+    split = q_heads * HD
+    y[:, :split] = y_part[:, :split] + jnp.dot(
+        normed, q_weight[part, :], preferred_element_type=jnp.float32
+    )
+    y[:, split:] = y_part[:, split:] + jnp.dot(
+        normed, kv_weight[part, :], preferred_element_type=jnp.float32
+    )
     per_kv = q_heads // kv_local
     length = mask.shape[1]
     for b in range(rows // length):
         here = slice(b * length, (b + 1) * length)
         row_scale = scale[here]
-        cosine = turn[here, :]
-        sine = cross[here, :]
-        visible = mask[here, :] > 0
+        there = slice(low + b * length, low + (b + 1) * length)
+        cosine = turn[there, :]
+        sine = cross[there, :]
+        visible = mask[there, :] > 0
 
         def rotated(value):
             return (value * cosine + pltpu.roll(value, HD // 2, 1) * sine).astype(jnp.bfloat16)
@@ -348,6 +443,14 @@
     return lax.ppermute(value, "mp", pairs)
 
 
+def table_values(length):
+    frequency = np.float32(rope_base) ** (-(np.arange(HD // 2, dtype=np.float32) * 2) / HD)
+    angles = np.arange(length, dtype=np.float32)[:, None] * frequency.astype(np.float32)
+    cosine, sine = np.cos(angles), np.sin(angles)
+    both = (np.concatenate([cosine, cosine], 1), np.concatenate([-sine, sine], 1))
+    return tuple(jnp.asarray(v, jnp.float32) for v in both)
+
+
 def line_device(hidden, segments, counts, dest_order, norm_gain, q_weight, kv_weight):
     n = lax.axis_size("dp")
     in_slots, block_len = segments.shape
@@ -360,30 +463,50 @@
     bf16 = jnp.bfloat16
     widths = tuple(local * e // 8 for e in FEATURE_EIGHTHS)
     dma = pltpu.SemaphoreType.DMA
-    heights = [block_len + (ID_ROWS if c == 0 else 0) for c in range(len(widths))]
-    packed = pl.pallas_call(
-        functools.partial(
-            pack_kernel, n=n, per_peer=per_peer, block_len=block_len, widths=widths
-        ),
-        out_shape=[
-            jax.ShapeDtypeStruct((n, per_peer, height, width), bf16)
-            for height, width in zip(heights, widths)
-        ],
-        in_specs=[SMEM, SMEM, VMEM, ANY],
-        out_specs=[VMEM] * len(widths),
-        scratch_shapes=[dma((len(widths), n, per_peer))],
-        name="pack",
-    )(counts, dest_order, segments, hidden)
+    packed = []
+    for c, width in enumerate(widths):
+        height = block_len + (ID_ROWS if c == 0 else 0)
+        scratch = [dma((n, per_peer))]
+        if c == 0:
+            scratch += [pltpu.VMEM(segments.shape, jnp.int32), dma(())]
+        operands = ([segments] if c == 0 else []) + [hidden]
+        packed.append(
+            pl.pallas_call(
+                functools.partial(
+                    pack_kernel,
+                    n=n,
+                    per_peer=per_peer,
+                    block_len=block_len,
+                    begin=sum(widths[:c]),
+                    width=width,
+                    with_ids=c == 0,
+                ),
+                out_shape=pltpu.VMEM((n, per_peer, height, width), bf16),
+                in_specs=[SMEM, SMEM] + [ANY] * len(operands),
+                out_specs=VMEM,
+                scratch_shapes=scratch,
+                compiler_params=limit(8),
+            )(*[afar(operand) for operand in [counts, dest_order] + operands])
+        )
+    q_near, kv_near = pl.pallas_call(
+        fetch_kernel,
+        out_shape=[pltpu.VMEM(w.shape, bf16) for w in (q_weight, kv_weight)],
+        in_specs=[ANY, ANY],
+        out_specs=[VMEM, VMEM],
+        scratch_shapes=[dma(()), dma(())],
+        compiler_params=limit(4),
+        name="fetch",
+    )(afar(q_weight), afar(kv_weight))
     came = []
     for buffer in packed:
         came.append(lax.all_to_all(buffer, "dp", split_axis=0, concat_axis=0, tiled=True))
     gathered = []
     block_ids = None
     for c, (width, arrived) in enumerate(zip(widths, came)):
-        groups = (kept,) if c == 0 else GROUPS
-        shapes = [jax.ShapeDtypeStruct((size * block_len, width), bf16) for size in groups]
+        groups = GROUPS if c == len(widths) - 1 else (kept,)
+        shapes = [pltpu.VMEM((size * block_len, width), bf16) for size in groups]
         if c == 0:
-            shapes.append(jax.ShapeDtypeStruct((kept, ID_ROWS, block_len), bf16))
+            shapes.append(pltpu.VMEM((kept, ID_ROWS, block_len), bf16))
         placed = pl.pallas_call(
             functools.partial(
                 place_kernel, n=n, block_len=block_len, groups=groups, with_ids=c == 0
@@ -391,9 +514,10 @@
             out_shape=shapes,
             in_specs=[SMEM, SMEM, VMEM],
             out_specs=[VMEM] * len(shapes),
-        )(counts, dest_order, arrived)
+            compiler_params=limit(4),
+        )(afar(counts), afar(dest_order), resident(arrived))
         if c == 0:
-            block_ids = placed[-1][:, 0, :]
+            block_ids = placed[-1]
             placed = placed[:-1]
         rows = []
         for own in placed:
@@ -404,54 +528,73 @@
             end_far = send(far, OUTWARD)
             rows.append([own, near, mid, far, end_mid, end_far])
         gathered.append(rows)
-    positions, visible = segment_masks(block_ids)
-    cosine, sine = rope_tables(positions, HD)
-    turn = jnp.concatenate([cosine, cosine], axis=-1).reshape(tokens, HD)
-    cross = jnp.concatenate([-sine, sine], axis=-1).reshape(tokens, HD)
-    mask = visible.astype(jnp.float32).reshape(tokens, block_len)
+    cosine, sine = table_values(block_len)
+    turn, cross, mask = pl.pallas_call(
+        functools.partial(table_kernel, kept=kept, length=block_len),
+        out_shape=[pltpu.VMEM((tokens, HD), jnp.float32)] * 2
+        + [pltpu.VMEM((tokens, block_len), jnp.float32)],
+        in_specs=[VMEM] * 3,
+        out_specs=[VMEM] * 3,
+        compiler_params=limit(4),
+        name="tables",
+    )(resident(block_ids), resident(cosine), resident(sine))
     gain = norm_gain[None, :]
+    columns = q_weight.shape[1] + kv_weight.shape[1]
+    last = len(widths) - 1
     out = None
     low = 0
     for g, size in enumerate(GROUPS):
         rows = size * block_len
         pieces, first_rows = [], []
         for c in range(len(widths)):
-            whole = len(gathered[c]) == 1
-            pieces += gathered[c][0 if whole else g]
+            whole = c < last
+            own, near, mid, far, end_mid, end_far = gathered[c][0 if whole else g]
+            pieces += [own, near, mid, end_mid] + ([far, end_far] if whole else [])
             first_rows.append(low if whole else None)
-        kernel = functools.partial(
-            layer_kernel,
-            widths=widths,
-            rows=rows,
-            low=low,
-            q_heads=q_heads,
-            kv_local=kv_local,
-            first_rows=tuple(first_rows),
-            fresh=out is None,
-        )
-        part = slice(low, low + rows)
-        operands = pieces + [gain, turn[part], cross[part], mask[part], q_weight, kv_weight]
+        operands = pieces + [gain, q_near, kv_near]
+        flops = 2 * rows * q_weight.shape[0] * columns
+        y, squares = pl.pallas_call(
+            functools.partial(project_kernel, widths=widths, first_rows=tuple(first_rows)),
+            out_shape=[
+                pltpu.VMEM((rows, columns), jnp.float32),
+                pltpu.VMEM((rows, HD), jnp.float32),
+            ],
+            in_specs=[VMEM] * len(operands),
+            out_specs=[VMEM] * 2,
+            scratch_shapes=[pltpu.VMEM((rows, 4 * local), bf16)],
+            compiler_params=limit(12),
+            cost_estimate=pl.CostEstimate(flops=flops, transcendentals=0, bytes_accessed=16 * MIB),
+        )(*[resident(operand) for operand in operands])
+        operands = [far, end_far, y, squares, gain, turn, cross, mask, q_near, kv_near]
+        operands = [resident(operand) for operand in operands]
         specs = [VMEM] * len(operands)
         aliases = {}
         if out is not None:
             aliases = {len(operands): 0}
             operands.append(out)
             specs.append(ANY)
-        flops = 2 * rows * q_weight.shape[0] * (q_weight.shape[1] + kv_weight.shape[1])
         out = pl.pallas_call(
-            kernel,
+            functools.partial(
+                attend_kernel,
+                first=sum(widths[:last]),
+                low=low,
+                q_heads=q_heads,
+                kv_local=kv_local,
+                fresh=out is None,
+            ),
             out_shape=jax.ShapeDtypeStruct((tokens, q_heads * HD), bf16),
             in_specs=specs,
             out_specs=ANY,
             input_output_aliases=aliases,
             scratch_shapes=[
-                pltpu.VMEM((rows, 4 * local), bf16),
-                pltpu.VMEM((rows, q_weight.shape[1] + kv_weight.shape[1]), jnp.float32),
+                pltpu.VMEM((rows, widths[last]), bf16),
+                pltpu.VMEM((rows, columns), jnp.float32),
                 pltpu.VMEM((rows, q_heads * HD), bf16),
                 dma(()),
             ],
+            compiler_params=limit(12),
             cost_estimate=pl.CostEstimate(
-                flops=flops, transcendentals=0, bytes_accessed=16 * 1024 * 1024
+                flops=flops // 4, transcendentals=0, bytes_accessed=4 * MIB
             ),
         )(*operands)
         low += rows

time: 195 us -> 209 us (1.072)
  the two profiles are of different devices: /device:TPU:16 before, /device:TPU:0 now
where the time goes in v2:
time: 209 us; the launch traced here: 208 us
  waiting for transfers between devices  110 us (53%)
  starting transfers between devices  56.1 us (27%)
  Pallas kernels  41.2 us (20%)
    ppermute x25, waiting for transfers between devices, send(): return lax.ppermute(value, 'mp', pairs)  81.9 us
    ppermute x25, starting transfers between devices, send(): return lax.ppermute(value, 'mp', pairs)  46.4 us
    all_to_all x2, waiting for transfers between devices, line_device(): lax.all_to_all(buffer, 'dp', split_axis=0, concat_axis=0, tiled=True)  28.5 us
    pallas_call x4, Pallas kernels, line_device(): pl.pallas_call(functools.partial(project_kernel, widths=widths, first_row...  14.4 us
    pallas_call x4, Pallas kernels, line_device(): pl.pallas_call(functools.partial(attend_kernel, first=sum(widths[:last]),...  10.4 us
    all_to_all x2, starting transfers between devices, line_device(): lax.all_to_all(buffer, 'dp', split_axis=0, concat_axis=0, tiled=True)  9.61 us
    pallas_call x2, Pallas kernels, line_device(): pl.pallas_call(functools.partial(pack_kernel, n=n, per_peer=per_peer, blo...  7.69 us
    pallas_call x1, Pallas kernels, line_device(): pl.pallas_call(fetch_kernel, out_shape=[pltpu.VMEM(w.shape, bf16) for w i...  4.63 us
  transfers between devices with their start and end apart: 27, of which 11 were waited for; matrix products, arithmetic and copies ran while one was open for 0% of the time, Pallas kernels for 17%

profile of v2, /device:TPU:0, one launch (start us, length us, event | category | flops | bytes accessed | tf_op | source)
XLA Modules:
  0.0 208.4 jit_solution(10211237694152874595)
XLA Ops:
  0.0 3.5 %shard_map.93 = bf16[8,2,136,384]{3,2,1,0:T(8,128)(2,1)} custom-call(s32[8]{0:T(128)} %counts.7, s32[8]{0:T(128)} %dest_order.7, s32[16,128]{1,0:T(8,128)} %refs_0_.3, bf16[2048,1024]{1,0:T(8,128)(2,1)} %refs_1_.1), custom_call_target="tpu_custom_call" | custom-call | tf_op jit(solution)/shard_map/pallas_call | solution.py:474
  3.5 5.2 %all-to-all-start.1 = ((bf16[8,2,136,384]{3,2,1,0:T(8,128)(2,1)}), bf16[8,2,136,384]{3,2,1,0:T(8,128)(2,1)S(1)}, u32[]{:S(2)}, u32[]{:S(2)}) async-start(bf16[8,2,136,384]{3,2,1,0:T(8,128)(2,1)} %shard_map.93), calls=%async_computation.1 | async-start | bytes 3342336 | tf_op jit(solution)/shard_map/all_to_all | solution.py:502
  8.7 4.2 %shard_map.91 = bf16[8,2,128,640]{3,2,1,0:T(8,128)(2,1)} custom-call(s32[8]{0:T(128)} %counts.7, s32[8]{0:T(128)} %dest_order.7, bf16[2048,1024]{1,0:T(8,128)(2,1)} %refs_1_.1), custom_call_target="tpu_custom_call" | custom-call | tf_op jit(solution)/shard_map/pallas_call | solution.py:474
  12.9 17.9 %all-to-all-done.1.arrived = bf16[8,2,136,384]{3,2,1,0:T(8,128)(2,1)S(1)} async-done(((bf16[8,2,136,384]{3,2,1,0:T(8,128)(2,1)}), bf16[8,2,136,384]{3,2,1,0:T(8,128)(2,1)S(1)}, u32[]{:S(2)}, u32[]{:S(2)}) %all-to-all-start.1) | async-done | bytes 1671200 | tf_op jit(solution)/shard_map/all_to_all | solution.py:502
  30.8 4.4 %all-to-all-start = ((bf16[8,2,128,640]{3,2,1,0:T(8,128)(2,1)}), bf16[8,2,128,640]{3,2,1,0:T(8,128)(2,1)}, u32[]{:S(2)}, u32[]{:S(2)}) async-start(bf16[8,2,128,640]{3,2,1,0:T(8,128)(2,1)} %shard_map.91), calls=%async_computation | async-start | bytes 5242880 | tf_op jit(solution)/shard_map/all_to_all | solution.py:502
  35.2 1.0 shard_map.94
  36.2 1.6 collective-permute-start.3
  37.8 0.7 collective-permute-start.4
  38.5 17.5 %collective-permute-done.3.refs_1_ = bf16[1024,384]{1,0:T(8,128)(2,1)S(1)} collective-permute-done((bf16[1024,384]{1,0:T(8,128)(2,1)S(1)}, bf16[1024,384]{1,0:T(8,128)(2,1)S(1)}, u32[]{:S(2)}, u32[]{:S(2)}) %collective-permute-start.3) | collective-permute-done | bytes 786464 | tf_op jit(solution)/shard_map/ppermute | solution.py:443
  56.1 0.7 collective-permute-start.6
  56.8 10.7 %all-to-all-done.arrived = bf16[8,2,128,640]{3,2,1,0:T(8,128)(2,1)} async-done(((bf16[8,2,128,640]{3,2,1,0:T(8,128)(2,1)}), bf16[8,2,128,640]{3,2,1,0:T(8,128)(2,1)}, u32[]{:S(2)}, u32[]{:S(2)}) %all-to-all-start) | async-done | bytes 2621472 | tf_op jit(solution)/shard_map/all_to_all | solution.py:502
  67.4 1.9 shard_map.92
  70.0 0.7 collective-permute-start.18
  70.7 0.7 collective-permute-start.23
  71.4 8.9 %collective-permute-start = (bf16[128,640]{1,0:T(8,128)(2,1)S(1)}, bf16[128,640]{1,0:T(8,128)(2,1)S(1)}, u32[]{:S(2)}, u32[]{:S(2)}) collective-permute-start(bf16[128,640]{1,0:T(8,128)(2,1)S(1)} %get-tuple-element.24.refs_6_), channel_id=1, source_target_pairs={{0,1},{1,0},{2,3},{3,2},{4,5},{5,4},{6,7},{7,6},{8,9},{9,8},{10,11... | collective-permute-start | bytes 491528 | tf_op jit(solution)/shard_map/ppermute | solution.py:443
  80.4 3.1 %collective-permute-start.15 = (bf16[256,640]{1,0:T(8,128)(2,1)S(1)}, bf16[256,640]{1,0:T(8,128)(2,1)S(1)}, u32[]{:S(2)}, u32[]{:S(2)}) collective-permute-start(bf16[256,640]{1,0:T(8,128)(2,1)S(1)} %get-tuple-element.37.refs_6_), channel_id=1, source_target_pairs={{0,1},{1,0},{2,3},{3,2},{4,5},{5,4},{6,7},{7,6},{8,9},{9,8},{10,11... | collective-permute-start | bytes 983048 | tf_op jit(solution)/shard_map/ppermute | solution.py:443
  83.4 2.0 collective-permute-done.refs_7_
  85.4 1.3 collective-permute-start.5
  86.7 1.3 collective-permute-start.7
  88.0 0.7 collective-permute-start.13
  88.7 3.7 %collective-permute-done.15.refs_7_ = bf16[256,640]{1,0:T(8,128)(2,1)S(1)} collective-permute-done((bf16[256,640]{1,0:T(8,128)(2,1)S(1)}, bf16[256,640]{1,0:T(8,128)(2,1)S(1)}, u32[]{:S(2)}, u32[]{:S(2)}) %collective-permute-start.15) | collective-permute-done | bytes 327712 | tf_op jit(solution)/shard_map/ppermute | solution.py:443
  92.4 1.6 collective-permute-start.20
  94.0 1.3 collective-permute-start.24
  95.3 11.3 %collective-permute-start.10 = (bf16[256,640]{1,0:T(8,128)(2,1)S(1)}, bf16[256,640]{1,0:T(8,128)(2,1)S(1)}, u32[]{:S(2)}, u32[]{:S(2)}) collective-permute-start(bf16[256,640]{1,0:T(8,128)(2,1)S(1)} %get-tuple-element.34.refs_6_), channel_id=1, source_target_pairs={{0,1},{1,0},{2,3},{3,2},{4,5},{5,4},{6,7},{7,6},{8,9},{9,8},{10,11... | collective-permute-start | bytes 983048 | tf_op jit(solution)/shard_map/ppermute | solution.py:443
  106.7 30.0 %collective-permute-done.20.refs_7_ = bf16[384,640]{1,0:T(8,128)(2,1)S(1)} collective-permute-done((bf16[384,640]{1,0:T(8,128)(2,1)S(1)}, bf16[384,640]{1,0:T(8,128)(2,1)S(1)}, u32[]{:S(2)}, u32[]{:S(2)}) %collective-permute-start.20) | collective-permute-done | bytes 491552 | tf_op jit(solution)/shard_map/ppermute | solution.py:443
  137.4 4.6 %fetch.1 = (bf16[4096,1024]{1,0:T(8,128)(2,1)S(1)}, bf16[4096,512]{1,0:T(8,128)(2,1)S(1)}) custom-call(bf16[4096,1024]{1,0:T(8,128)(2,1)} %q_weight.1, bf16[4096,512]{1,0:T(8,128)(2,1)} %kv_weight.1), custom_call_target="tpu_custom_call" | custom-call | tf_op jit(solution)/shard_map/fetch/pallas_call | solution.py:491
  142.1 1.2 tables.1
  143.3 9.0 %collective-permute-done.10.refs_7_ = bf16[256,640]{1,0:T(8,128)(2,1)S(1)} collective-permute-done((bf16[256,640]{1,0:T(8,128)(2,1)S(1)}, bf16[256,640]{1,0:T(8,128)(2,1)S(1)}, u32[]{:S(2)}, u32[]{:S(2)}) %collective-permute-start.10) | collective-permute-done | bytes 327712 | tf_op jit(solution)/shard_map/ppermute | solution.py:443
  152.3 1.3 collective-permute-start.19
  153.6 0.7 collective-permute-start.16
  154.3 1.3 collective-permute-start.14
  156.3 5.3 %shard_map.98 = (f32[384,1536]{1,0:T(8,128)S(1)}, f32[384,128]{1,0:T(8,128)S(1)}) custom-call(bf16[1024,384]{1,0:T(8,128)(2,1)S(1)} %get-tuple-element.25.refs_0_, bf16[1024,384]{1,0:T(8,128)(2,1)S(1)} %collective-permute-done.3.refs_1_, bf16[1024,384]{1,0:T(8,128)(2,1)S(1)} %collective-permute-done.4.refs_2_, ...), custom_call_target="tpu_custom_call" | custom-call | flops 4831838208 | bytes 16777216 | tf_op jit(solution)/shard_map/pallas_call | solution.py:556
  161.6 3.1 %collective-permute-done.19.refs_9_ = bf16[256,640]{1,0:T(8,128)(2,1)S(1)} collective-permute-done((bf16[256,640]{1,0:T(8,128)(2,1)S(1)}, bf16[256,640]{1,0:T(8,128)(2,1)S(1)}, u32[]{:S(2)}, u32[]{:S(2)}) %collective-permute-start.19) | collective-permute-done | bytes 327712 | tf_op jit(solution)/shard_map/ppermute | solution.py:443
  165.4 1.3 collective-permute-start.22
  166.7 3.6 %shard_map.97 = (f32[256,1536]{1,0:T(8,128)S(1)}, f32[256,128]{1,0:T(8,128)S(1)}) custom-call(bf16[1024,384]{1,0:T(8,128)(2,1)S(1)} %get-tuple-element.25.refs_0_, bf16[1024,384]{1,0:T(8,128)(2,1)S(1)} %collective-permute-done.3.refs_1_, bf16[1024,384]{1,0:T(8,128)(2,1)S(1)} %collective-permute-done.4.refs_2_, ...), custom_call_target="tpu_custom_call" | custom-call | flops 3221225472 | bytes 16777216 | tf_op jit(solution)/shard_map/pallas_call | solution.py:556
  170.3 1.5 collective-permute-start.9
  171.8 1.3 collective-permute-start.2
  173.1 1.3 collective-permute-start.17
  174.4 1.3 collective-permute-start.12
  175.7 3.6 %shard_map.96 = (f32[256,1536]{1,0:T(8,128)S(1)}, f32[256,128]{1,0:T(8,128)S(1)}) custom-call(bf16[1024,384]{1,0:T(8,128)(2,1)S(1)} %get-tuple-element.25.refs_0_, bf16[1024,384]{1,0:T(8,128)(2,1)S(1)} %collective-permute-done.3.refs_1_, bf16[1024,384]{1,0:T(8,128)(2,1)S(1)} %collective-permute-done.4.refs_2_, ...), custom_call_target="tpu_custom_call" | custom-call | flops 3221225472 | bytes 16777216 | tf_op jit(solution)/shard_map/pallas_call | solution.py:556
  179.3 5.4 %collective-permute-done.22.refs_1_ = bf16[384,640]{1,0:T(8,128)(2,1)S(1)} collective-permute-done((bf16[384,640]{1,0:T(8,128)(2,1)S(1)}, bf16[384,640]{1,0:T(8,128)(2,1)S(1)}, u32[]{:S(2)}, u32[]{:S(2)}) %collective-permute-start.22) | collective-permute-done | bytes 491552 | tf_op jit(solution)/shard_map/ppermute | solution.py:443
  184.7 3.3 %shard_map.99.refs_10_ = bf16[1024,1024]{1,0:T(8,128)(2,1)} custom-call(bf16[384,640]{1,0:T(8,128)(2,1)S(1)} %collective-permute-done.21.refs_0_, bf16[384,640]{1,0:T(8,128)(2,1)S(1)} %collective-permute-done.22.refs_1_, f32[384,1536]{1,0:T(8,128)S(1)} %get-tuple-element.41.refs_2_, f32[384,128]{1,0:T(8,128)S(1)} %get-tuple-element.42.refs_3_, ...), custom_call_target="tpu_custom_call" | custom-call | flops 1207959552 | bytes 4194304 | tf_op jit(solution)/shard_map/pallas_call | solution.py:576
  188.0 10.2 %collective-permute-done.17.refs_1_ = bf16[256,640]{1,0:T(8,128)(2,1)S(1)} collective-permute-done((bf16[256,640]{1,0:T(8,128)(2,1)S(1)}, bf16[256,640]{1,0:T(8,128)(2,1)S(1)}, u32[]{:S(2)}, u32[]{:S(2)}) %collective-permute-start.17) | collective-permute-done | bytes 327712 | tf_op jit(solution)/shard_map/ppermute | solution.py:443
  198.2 2.6 %shard_map.100.refs_10_ = bf16[1024,1024]{1,0:T(8,128)(2,1)} custom-call(bf16[256,640]{1,0:T(8,128)(2,1)S(1)} %collective-permute-done.16.refs_0_, bf16[256,640]{1,0:T(8,128)(2,1)S(1)} %collective-permute-done.17.refs_1_, f32[256,1536]{1,0:T(8,128)S(1)} %get-tuple-element.38.refs_2_, ...), custom_call_target="tpu_custom_call", output_to_operand_aliasing={{}: (10, {})} | custom-call | flops 805306368 | bytes 4194304 | tf_op jit(solution)/shard_map/pallas_call | solution.py:576
  200.8 0.9 collective-permute-done.12.refs_1_
  201.7 2.6 %shard_map.101.refs_10_ = bf16[1024,1024]{1,0:T(8,128)(2,1)} custom-call(bf16[256,640]{1,0:T(8,128)(2,1)S(1)} %collective-permute-done.11.refs_0_, bf16[256,640]{1,0:T(8,128)(2,1)S(1)} %collective-permute-done.12.refs_1_, f32[256,1536]{1,0:T(8,128)S(1)} %get-tuple-element.35.refs_2_, ...), custom_call_target="tpu_custom_call", output_to_operand_aliasing={{}: (10, {})} | custom-call | flops 805306368 | bytes 4194304 | tf_op jit(solution)/shard_map/pallas_call | solution.py:576
  204.3 1.9 shard_map.95
  206.3 1.9 shard_map.102
  (27 shorter events, 2.8 us)
Async XLA Ops:
  3.5 27.3 %all-to-all-start.1 = ((bf16[8,2,136,384]{3,2,1,0:T(8,128)(2,1)}), bf16[8,2,136,384]{3,2,1,0:T(8,128)(2,1)S(1)}, u32[]{:S(2)}, u32[]{:S(2)}) async-start(bf16[8,2,136,384]{3,2,1,0:T(8,128)(2,1)} %shard_map.93), calls=%async_computation.1 | async-start | bytes 3342336 | tf_op jit(solution)/shard_map/all_to_all | solution.py:502
  30.8 36.7 %all-to-all-start = ((bf16[8,2,128,640]{3,2,1,0:T(8,128)(2,1)}), bf16[8,2,128,640]{3,2,1,0:T(8,128)(2,1)}, u32[]{:S(2)}, u32[]{:S(2)}) async-start(bf16[8,2,128,640]{3,2,1,0:T(8,128)(2,1)} %shard_map.91), calls=%async_computation | async-start | bytes 5242880 | tf_op jit(solution)/shard_map/all_to_all | solution.py:502
  35.2 102.2 %copy-start.2 = (bf16[4096]{0:T(1024)(128)(2,1)S(1)}, bf16[4096]{0:T(1024)(128)(2,1)}, u32[]{:S(2)}) copy-start(bf16[4096]{0:T(1024)(128)(2,1)} %param.13) | copy-start | bytes 24580
  36.2 19.9 %collective-permute-start.3 = (bf16[1024,384]{1,0:T(8,128)(2,1)S(1)}, bf16[1024,384]{1,0:T(8,128)(2,1)S(1)}, u32[]{:S(2)}, u32[]{:S(2)}) collective-permute-start(bf16[1024,384]{1,0:T(8,128)(2,1)S(1)} %get-tuple-element.25.refs_0_), channel_id=1, source_target_pairs={{0,1},{1,0},{2,3},{3,2},{4,5},{5,4},{6,7},{7,6},{8,9},{9,8},{10,11... | collective-permute-start | bytes 2359304 | tf_op jit(solution)/shard_map/ppermute | solution.py:443
  37.8 33.6 %collective-permute-start.4 = (bf16[1024,384]{1,0:T(8,128)(2,1)S(1)}, bf16[1024,384]{1,0:T(8,128)(2,1)S(1)}, u32[]{:S(2)}, u32[]{:S(2)}) collective-permute-start(bf16[1024,384]{1,0:T(8,128)(2,1)S(1)} %get-tuple-element.25.refs_0_), channel_id=1, source_target_pairs={{1,2},{2,1},{5,6},{6,5},{9,10},{10,9},{13,14},{14,13},{17,18},{18,... | collective-permute-start | bytes 2359304 | tf_op jit(solution)/shard_map/ppermute | solution.py:443
  56.1 30.7 %collective-permute-start.6 = (bf16[1024,384]{1,0:T(8,128)(2,1)S(1)}, bf16[1024,384]{1,0:T(8,128)(2,1)S(1)}, u32[]{:S(2)}, u32[]{:S(2)}) collective-permute-start(bf16[1024,384]{1,0:T(8,128)(2,1)S(1)} %collective-permute-done.3.refs_1_), channel_id=1, source_target_pairs={{1,2},{2,1},{5,6},{6,5},{9,10},{10,9},{13,14},{14,13},{17,18},{18,... | collective-permute-start | bytes 2359304 | tf_op jit(solution)/shard_map/ppermute | solution.py:443
  69.4 11.0 %collective-permute-start.8 = (bf16[128,640]{1,0:T(8,128)(2,1)S(1)}, bf16[128,640]{1,0:T(8,128)(2,1)S(1)}, u32[]{:S(2)}, u32[]{:S(2)}) collective-permute-start(bf16[128,640]{1,0:T(8,128)(2,1)S(1)} %get-tuple-element.24.refs_6_), channel_id=1, source_target_pairs={{1,2},{2,1},{5,6},{6,5},{9,10},{10,9},{13,14},{14,13},{17,18},{18,... | collective-permute-start | bytes 491528 | tf_op jit(solution)/shard_map/ppermute | solution.py:443
  70.0 18.0 %collective-permute-start.18 = (bf16[256,640]{1,0:T(8,128)(2,1)S(1)}, bf16[256,640]{1,0:T(8,128)(2,1)S(1)}, u32[]{:S(2)}, u32[]{:S(2)}) collective-permute-start(bf16[256,640]{1,0:T(8,128)(2,1)S(1)} %get-tuple-element.37.refs_6_), channel_id=1, source_target_pairs={{1,2},{2,1},{5,6},{6,5},{9,10},{10,9},{13,14},{14,13},{17,18},{18,... | collective-permute-start | bytes 983048 | tf_op jit(solution)/shard_map/ppermute | solution.py:443
  70.7 23.3 %collective-permute-start.23 = (bf16[384,640]{1,0:T(8,128)(2,1)S(1)}, bf16[384,640]{1,0:T(8,128)(2,1)S(1)}, u32[]{:S(2)}, u32[]{:S(2)}) collective-permute-start(bf16[384,640]{1,0:T(8,128)(2,1)S(1)} %get-tuple-element.40.refs_6_), channel_id=1, source_target_pairs={{1,2},{2,1},{5,6},{6,5},{9,10},{10,9},{13,14},{14,13},{17,18},{18,... | collective-permute-start | bytes 1474568 | tf_op jit(solution)/shard_map/ppermute | solution.py:443
  71.4 14.0 %collective-permute-start = (bf16[128,640]{1,0:T(8,128)(2,1)S(1)}, bf16[128,640]{1,0:T(8,128)(2,1)S(1)}, u32[]{:S(2)}, u32[]{:S(2)}) collective-permute-start(bf16[128,640]{1,0:T(8,128)(2,1)S(1)} %get-tuple-element.24.refs_6_), channel_id=1, source_target_pairs={{0,1},{1,0},{2,3},{3,2},{4,5},{5,4},{6,7},{7,6},{8,9},{9,8},{10,11... | collective-permute-start | bytes 491528 | tf_op jit(solution)/shard_map/ppermute | solution.py:443
  80.4 12.1 %collective-permute-start.15 = (bf16[256,640]{1,0:T(8,128)(2,1)S(1)}, bf16[256,640]{1,0:T(8,128)(2,1)S(1)}, u32[]{:S(2)}, u32[]{:S(2)}) collective-permute-start(bf16[256,640]{1,0:T(8,128)(2,1)S(1)} %get-tuple-element.37.refs_6_), channel_id=1, source_target_pairs={{0,1},{1,0},{2,3},{3,2},{4,5},{5,4},{6,7},{7,6},{8,9},{9,8},{10,11... | collective-permute-start | bytes 983048 | tf_op jit(solution)/shard_map/ppermute | solution.py:443
  85.4 68.1 %collective-permute-start.5 = (bf16[1024,384]{1,0:T(8,128)(2,1)S(1)}, bf16[1024,384]{1,0:T(8,128)(2,1)S(1)}, u32[]{:S(2)}, u32[]{:S(2)}) collective-permute-start(bf16[1024,384]{1,0:T(8,128)(2,1)S(1)} %collective-permute-done.4.refs_2_), channel_id=1, source_target_pairs={{1,0},{2,3},{5,4},{6,7},{9,8},{10,11},{13,12},{14,15},{17,16},{18,... | collective-permute-start | bytes 2359304 | tf_op jit(solution)/shard_map/ppermute | solution.py:443
  86.7 68.8 %collective-permute-start.7 = (bf16[1024,384]{1,0:T(8,128)(2,1)S(1)}, bf16[1024,384]{1,0:T(8,128)(2,1)S(1)}, u32[]{:S(2)}, u32[]{:S(2)}) collective-permute-start(bf16[1024,384]{1,0:T(8,128)(2,1)S(1)} %collective-permute-done.6.refs_4_), channel_id=1, source_target_pairs={{1,0},{2,3},{5,4},{6,7},{9,8},{10,11},{13,12},{14,15},{17,16},{18,... | collective-permute-start | bytes 2359304 | tf_op jit(solution)/shard_map/ppermute | solution.py:443
  88.0 7.3 %collective-permute-start.13 = (bf16[256,640]{1,0:T(8,128)(2,1)S(1)}, bf16[256,640]{1,0:T(8,128)(2,1)S(1)}, u32[]{:S(2)}, u32[]{:S(2)}) collective-permute-start(bf16[256,640]{1,0:T(8,128)(2,1)S(1)} %get-tuple-element.34.refs_6_), channel_id=1, source_target_pairs={{1,2},{2,1},{5,6},{6,5},{9,10},{10,9},{13,14},{14,13},{17,18},{18,... | collective-permute-start | bytes 983048 | tf_op jit(solution)/shard_map/ppermute | solution.py:443
  92.4 44.2 %collective-permute-start.20 = (bf16[384,640]{1,0:T(8,128)(2,1)S(1)}, bf16[384,640]{1,0:T(8,128)(2,1)S(1)}, u32[]{:S(2)}, u32[]{:S(2)}) collective-permute-start(bf16[384,640]{1,0:T(8,128)(2,1)S(1)} %get-tuple-element.40.refs_6_), channel_id=1, source_target_pairs={{0,1},{1,0},{2,3},{3,2},{4,5},{5,4},{6,7},{7,6},{8,9},{9,8},{10,11... | collective-permute-start | bytes 1474568 | tf_op jit(solution)/shard_map/ppermute | solution.py:443
  94.0 60.2 %collective-permute-start.24 = (bf16[384,640]{1,0:T(8,128)(2,1)S(1)}, bf16[384,640]{1,0:T(8,128)(2,1)S(1)}, u32[]{:S(2)}, u32[]{:S(2)}) collective-permute-start(bf16[384,640]{1,0:T(8,128)(2,1)S(1)} %collective-permute-done.23.refs_8_), channel_id=1, source_target_pairs={{1,0},{2,3},{5,4},{6,7},{9,8},{10,11},{13,12},{14,15},{17,16},{18,... | collective-permute-start | bytes 1474568 | tf_op jit(solution)/shard_map/ppermute | solution.py:443
  95.3 56.9 %collective-permute-start.10 = (bf16[256,640]{1,0:T(8,128)(2,1)S(1)}, bf16[256,640]{1,0:T(8,128)(2,1)S(1)}, u32[]{:S(2)}, u32[]{:S(2)}) collective-permute-start(bf16[256,640]{1,0:T(8,128)(2,1)S(1)} %get-tuple-element.34.refs_6_), channel_id=1, source_target_pairs={{0,1},{1,0},{2,3},{3,2},{4,5},{5,4},{6,7},{7,6},{8,9},{9,8},{10,11... | collective-permute-start | bytes 983048 | tf_op jit(solution)/shard_map/ppermute | solution.py:443
  136.7 28.7 %collective-permute-start.21 = (bf16[384,640]{1,0:T(8,128)(2,1)S(1)}, bf16[384,640]{1,0:T(8,128)(2,1)S(1)}, u32[]{:S(2)}, u32[]{:S(2)}) collective-permute-start(bf16[384,640]{1,0:T(8,128)(2,1)S(1)} %collective-permute-done.20.refs_7_), channel_id=1, source_target_pairs={{1,2},{2,1},{5,6},{6,5},{9,10},{10,9},{13,14},{14,13},{17,18},{18,... | collective-permute-start | bytes 1474568 | tf_op jit(solution)/shard_map/ppermute | solution.py:443
  137.4 4.7 %copy-start = (f32[128,128]{1,0:T(8,128)S(1)}, f32[128,128]{1,0:T(8,128)}, u32[]{:S(2)}) copy-start(f32[128,128]{1,0:T(8,128)} %constant.4.clone.cosines) | copy-start | bytes 196612
  137.4 4.7 %copy-start.1 = (f32[128,128]{1,0:T(8,128)S(1)}, f32[128,128]{1,0:T(8,128)}, u32[]{:S(2)}) copy-start(f32[128,128]{1,0:T(8,128)} %constant.5.clone.sines) | copy-start | bytes 196612
  152.3 12.5 %collective-permute-start.19 = (bf16[256,640]{1,0:T(8,128)(2,1)S(1)}, bf16[256,640]{1,0:T(8,128)(2,1)S(1)}, u32[]{:S(2)}, u32[]{:S(2)}) collective-permute-start(bf16[256,640]{1,0:T(8,128)(2,1)S(1)} %collective-permute-done.18.refs_8_), channel_id=1, source_target_pairs={{1,0},{2,3},{5,4},{6,7},{9,8},{10,11},{13,12},{14,15},{17,16},{18,... | collective-permute-start | bytes 983048 | tf_op jit(solution)/shard_map/ppermute | solution.py:443
  153.6 18.2 %collective-permute-start.16 = (bf16[256,640]{1,0:T(8,128)(2,1)S(1)}, bf16[256,640]{1,0:T(8,128)(2,1)S(1)}, u32[]{:S(2)}, u32[]{:S(2)}) collective-permute-start(bf16[256,640]{1,0:T(8,128)(2,1)S(1)} %collective-permute-done.15.refs_7_), channel_id=1, source_target_pairs={{1,2},{2,1},{5,6},{6,5},{9,10},{10,9},{13,14},{14,13},{17,18},{18,... | collective-permute-start | bytes 983048 | tf_op jit(solution)/shard_map/ppermute | solution.py:443
  154.3 18.9 %collective-permute-start.14 = (bf16[256,640]{1,0:T(8,128)(2,1)S(1)}, bf16[256,640]{1,0:T(8,128)(2,1)S(1)}, u32[]{:S(2)}, u32[]{:S(2)}) collective-permute-start(bf16[256,640]{1,0:T(8,128)(2,1)S(1)} %collective-permute-done.13.refs_8_), channel_id=1, source_target_pairs={{1,0},{2,3},{5,4},{6,7},{9,8},{10,11},{13,12},{14,15},{17,16},{18,... | collective-permute-start | bytes 983048 | tf_op jit(solution)/shard_map/ppermute | solution.py:443
  155.6 18.9 %collective-permute-start.11 = (bf16[256,640]{1,0:T(8,128)(2,1)S(1)}, bf16[256,640]{1,0:T(8,128)(2,1)S(1)}, u32[]{:S(2)}, u32[]{:S(2)}) collective-permute-start(bf16[256,640]{1,0:T(8,128)(2,1)S(1)} %collective-permute-done.10.refs_7_), channel_id=1, source_target_pairs={{1,2},{2,1},{5,6},{6,5},{9,10},{10,9},{13,14},{14,13},{17,18},{18,... | collective-permute-start | bytes 983048 | tf_op jit(solution)/shard_map/ppermute | solution.py:443
  164.7 5.6 %collective-permute-start.1 = (bf16[128,640]{1,0:T(8,128)(2,1)S(1)}, bf16[128,640]{1,0:T(8,128)(2,1)S(1)}, u32[]{:S(2)}, u32[]{:S(2)}) collective-permute-start(bf16[128,640]{1,0:T(8,128)(2,1)S(1)} %collective-permute-done.refs_7_), channel_id=1, source_target_pairs={{1,2},{2,1},{5,6},{6,5},{9,10},{10,9},{13,14},{14,13},{17,18},{18,... | collective-permute-start | bytes 491528 | tf_op jit(solution)/shard_map/ppermute | solution.py:443
  165.4 19.3 %collective-permute-start.22 = (bf16[384,640]{1,0:T(8,128)(2,1)S(1)}, bf16[384,640]{1,0:T(8,128)(2,1)S(1)}, u32[]{:S(2)}, u32[]{:S(2)}) collective-permute-start(bf16[384,640]{1,0:T(8,128)(2,1)S(1)} %collective-permute-done.21.refs_0_), channel_id=1, source_target_pairs={{1,0},{2,3},{5,4},{6,7},{9,8},{10,11},{13,12},{14,15},{17,16},{18,... | collective-permute-start | bytes 1474568 | tf_op jit(solution)/shard_map/ppermute | solution.py:443
  170.3 34.0 %collective-permute-start.9 = (bf16[128,640]{1,0:T(8,128)(2,1)S(1)}, bf16[128,640]{1,0:T(8,128)(2,1)S(1)}, u32[]{:S(2)}, u32[]{:S(2)}) collective-permute-start(bf16[128,640]{1,0:T(8,128)(2,1)S(1)} %collective-permute-done.8.refs_8_), channel_id=1, source_target_pairs={{1,0},{2,3},{5,4},{6,7},{9,8},{10,11},{13,12},{14,15},{17,16},{18,... | collective-permute-start | bytes 491528 | tf_op jit(solution)/shard_map/ppermute | solution.py:443
  171.8 34.4 %collective-permute-start.2 = (bf16[128,640]{1,0:T(8,128)(2,1)S(1)}, bf16[128,640]{1,0:T(8,128)(2,1)S(1)}, u32[]{:S(2)}, u32[]{:S(2)}) collective-permute-start(bf16[128,640]{1,0:T(8,128)(2,1)S(1)} %collective-permute-done.1.refs_0_), channel_id=1, source_target_pairs={{1,0},{2,3},{5,4},{6,7},{9,8},{10,11},{13,12},{14,15},{17,16},{18,... | collective-permute-start | bytes 491528 | tf_op jit(solution)/shard_map/ppermute | solution.py:443
  173.1 25.1 %collective-permute-start.17 = (bf16[256,640]{1,0:T(8,128)(2,1)S(1)}, bf16[256,640]{1,0:T(8,128)(2,1)S(1)}, u32[]{:S(2)}, u32[]{:S(2)}) collective-permute-start(bf16[256,640]{1,0:T(8,128)(2,1)S(1)} %collective-permute-done.16.refs_0_), channel_id=1, source_target_pairs={{1,0},{2,3},{5,4},{6,7},{9,8},{10,11},{13,12},{14,15},{17,16},{18,... | collective-permute-start | bytes 983048 | tf_op jit(solution)/shard_map/ppermute | solution.py:443
  174.4 27.3 %collective-permute-start.12 = (bf16[256,640]{1,0:T(8,128)(2,1)S(1)}, bf16[256,640]{1,0:T(8,128)(2,1)S(1)}, u32[]{:S(2)}, u32[]{:S(2)}) collective-permute-start(bf16[256,640]{1,0:T(8,128)(2,1)S(1)} %collective-permute-done.11.refs_0_), channel_id=1, source_target_pairs={{1,0},{2,3},{5,4},{6,7},{9,8},{10,11},{13,12},{14,15},{17,16},{18,... | collective-permute-start | bytes 983048 | tf_op jit(solution)/shard_map/ppermute | solution.py:443

commit v3 on v2

--- a/solution.py
+++ b/solution.py
@@ -16,8 +16,8 @@
 rope_base = 500000.0
 
 ID_ROWS = 8
-FEATURE_EIGHTHS = (3, 5)
-GROUPS = (3, 2, 2, 1)
+FEATURE_EIGHTHS = (1, 2, 5)
+GROUPS = (3, 3, 2)
 
 
 def for_sending(array):
@@ -218,37 +218,39 @@
         fetch = pltpu.make_async_copy(segments, near, near_sem)
         fetch.start()
     else:
-        hidden, out, sems = refs
+        hidden, outs, sems = refs[0], refs[1 : n + 1], refs[n + 1]
     in_slots = hidden.shape[0] // block_len
     me = lax.axis_index("dp")
     mine = start_of(counts, me, n)
     slots = []
     copies = []
-    for peer in range(n):
+    for r in range(n):
+        peer = r if with_ids else lax.bitwise_xor(me, r)
         offset = lax.rem(place_of(dest_order, peer, n) - mine + n * in_slots, n)
         for a in range(per_peer):
             slot = jnp.minimum(offset + a * n, in_slots - 1)
             row = pl.multiple_of(slot * block_len, block_len)
+            target = out.at[r, a, pl.ds(0, block_len), :] if with_ids else outs[r].at[a]
             copies.append(
                 pltpu.make_async_copy(
-                    hidden.at[pl.ds(row, block_len), pl.ds(begin, width)],
-                    out.at[peer, a, pl.ds(0, block_len), :],
-                    sems.at[peer, a],
+                    hidden.at[pl.ds(row, block_len), pl.ds(begin, width)], target, sems.at[r, a]
                 )
             )
             copies[-1].start()
-            slots.append((peer, a, slot))
+            slots.append((r, a, slot))
     if with_ids:
         fetch.wait()
-        for peer, a, slot in slots:
+        for r, a, slot in slots:
             ids = near[pl.ds(slot, 1), :].astype(jnp.float32)
             ids = jnp.broadcast_to(ids, (ID_ROWS, block_len)).astype(jnp.bfloat16)
-            out[peer, a, block_len:, :block_len] = ids
+            out[r, a, block_len:, :block_len] = ids
     for copy in copies:
         copy.wait()
 
 
-def place_kernel(counts, dest_order, arrived, *outs, n, block_len, groups, with_ids):
+def place_kernel(counts, dest_order, *refs, n, block_len, groups, with_ids):
+    count = 1 if with_ids else n
+    arrived, outs = refs[:count], refs[count:]
     me = lax.axis_index("dp")
     my_place = place_of(dest_order, me, n)
     k = 0
@@ -264,9 +266,18 @@
                 source = source + passed.astype(jnp.int32)
                 begin = jnp.where(passed, total, begin)
             a = lax.div(wanted - begin, n)
-            outs[g][i * block_len : (i + 1) * block_len, :] = arrived[source, a, :block_len, :]
+            here = slice(i * block_len, (i + 1) * block_len)
             if with_ids:
-                outs[-1][k] = arrived[source, a, block_len:, :block_len]
+                outs[g][here, :] = arrived[0][source, a, :block_len, :]
+                outs[-1][k] = arrived[0][source, a, block_len:, :block_len]
+            else:
+                came_by = lax.bitwise_xor(source, me)
+                for r in range(n):
+
+                    @pl.when(came_by == r)
+                    def _():
+                        outs[g][here, :] = arrived[r][a]
+
             k += 1
 
 
@@ -481,9 +492,11 @@
                     width=width,
                     with_ids=c == 0,
                 ),
-                out_shape=pltpu.VMEM((n, per_peer, height, width), bf16),
+                out_shape=pltpu.VMEM((n, per_peer, height, width), bf16)
+                if c == 0
+                else [pltpu.VMEM((per_peer, height, width), bf16)] * n,
                 in_specs=[SMEM, SMEM] + [ANY] * len(operands),
-                out_specs=VMEM,
+                out_specs=VMEM if c == 0 else [VMEM] * n,
                 scratch_shapes=scratch,
                 compiler_params=limit(8),
             )(*[afar(operand) for operand in [counts, dest_order] + operands])
@@ -498,8 +511,14 @@
         name="fetch",
     )(afar(q_weight), afar(kv_weight))
     came = []
-    for buffer in packed:
-        came.append(lax.all_to_all(buffer, "dp", split_axis=0, concat_axis=0, tiled=True))
+    for c, buffers in enumerate(packed):
+        if c == 0:
+            came.append([lax.all_to_all(buffers, "dp", split_axis=0, concat_axis=0, tiled=True)])
+            continue
+        came.append([buffers[0]])
+        for r in range(1, n):
+            pairs = [(i, i ^ r) for i in range(n)]
+            came[-1].append(lax.ppermute(buffers[r], "dp", pairs))
     gathered = []
     block_ids = None
     for c, (width, arrived) in enumerate(zip(widths, came)):
@@ -512,10 +531,10 @@
                 place_kernel, n=n, block_len=block_len, groups=groups, with_ids=c == 0
             ),
             out_shape=shapes,
-            in_specs=[SMEM, SMEM, VMEM],
+            in_specs=[SMEM, SMEM] + [VMEM] * len(arrived),
             out_specs=[VMEM] * len(shapes),
             compiler_params=limit(4),
-        )(afar(counts), afar(dest_order), resident(arrived))
+        )(afar(counts), afar(dest_order), *[resident(part) for part in arrived])
         if c == 0:
             block_ids = placed[-1]
             placed = placed[:-1]
@@ -604,8 +623,8 @@
 def solution(mesh):
     in_specs = (P("dp", "mp"), P("dp", None), P(), P(), P(), P(None, "mp"), P(None, "mp"))
     out_specs = P("dp", "mp")
-    mp_count = mesh.shape["mp"]
-    line = mp_count == 4 and KV % mp_count == 0
+    dp_count, mp_count = mesh.shape["dp"], mesh.shape["mp"]
+    line = mp_count == 4 and dp_count == 8 and KV % mp_count == 0
 
     def body(*arrays):
         return line_device(*arrays)

time: 209 us -> 210 us (level)
  local copies, waits for them, and re-layouts: 0.03 us -> 9.53 us
  starting transfers between devices: 56.1 us -> 48.5 us
  waiting for transfers between devices: 110 us -> 106 us
  Pallas kernels: 41.2 us -> 44.4 us
    all_to_all x2 -> x1, waiting for transfers between devices: 28.5 us -> 0.01 us  [line_device(): lax.all_to_all(buffers, 'dp', split_axis=0, concat_axis=0, tiled=True)]
    ppermute x0 -> x14, waiting for transfers between devices: none -> 28.3 us  [line_device(): came[-1].append(lax.ppermute(buffers[r], 'dp', pairs))]
    ppermute x25, starting transfers between devices: 46.4 us -> 31.5 us  [send(): return lax.ppermute(value, 'mp', pairs)]
    ppermute x0 -> x14, starting transfers between devices: none -> 13 us  [line_device(): came[-1].append(lax.ppermute(buffers[r], 'dp', pairs))]
    unnamed x6 -> x34, local copies, waits for them, and re-layouts: 0.02 us -> 9.52 us
    all_to_all x2 -> x1, starting transfers between devices: 9.61 us -> 3.96 us  [line_device(): lax.all_to_all(buffers, 'dp', split_axis=0, concat_axis=0, tiled=True)]
    ppermute x25, waiting for transfers between devices: 81.9 us -> 77.8 us  [send(): return lax.ppermute(value, 'mp', pairs)]
    pallas_call x2 -> x3, Pallas kernels: 7.69 us -> 9.41 us  [line_device(): pl.pallas_call(functools.partial(pack_kernel, n=n, per_peer=per_peer, blo...]
  transfers between devices with their start and end apart: 27 -> 40, of which waited for: 11 -> 11; matrix products, arithmetic and copies ran while one was open for 0% -> 0% of each run, Pallas kernels for 17% -> 19%
where the time goes in v3:
time: 210 us; the launch traced here: 209 us
  waiting for transfers between devices  106 us (50%)
  starting transfers between devices  48.5 us (23%)
  Pallas kernels  44.4 us (21%)
  local copies, waits for them, and re-layouts  9.53 us (5%)
    ppermute x25, waiting for transfers between devices, send(): return lax.ppermute(value, 'mp', pairs)  77.8 us
    ppermute x25, starting transfers between devices, send(): return lax.ppermute(value, 'mp', pairs)  31.5 us
    ppermute x14, waiting for transfers between devices, line_device(): came[-1].append(lax.ppermute(buffers[r], 'dp', pairs))  28.3 us
    pallas_call x3, Pallas kernels, line_device(): pl.pallas_call(functools.partial(project_kernel, widths=widths, first_row...  15.8 us
    ppermute x14, starting transfers between devices, line_device(): came[-1].append(lax.ppermute(buffers[r], 'dp', pairs))  13 us
    unnamed x34, local copies, waits for them, and re-layouts  9.52 us
    pallas_call x3, Pallas kernels, line_device(): pl.pallas_call(functools.partial(pack_kernel, n=n, per_peer=per_peer, blo...  9.41 us
    pallas_call x3, Pallas kernels, line_device(): pl.pallas_call(functools.partial(attend_kernel, first=sum(widths[:last]),...  9.33 us
  transfers between devices with their start and end apart: 40, of which 11 were waited for; matrix products, arithmetic and copies ran while one was open for 0% of the time, Pallas kernels for 19%

profile of v3, /device:TPU:0, one launch (start us, length us, event | category | flops | bytes accessed | tf_op | source)
XLA Modules:
  0.0 209.2 jit_solution(17794425815476438187)
XLA Ops:
  0.0 2.8 %shard_map.95 = (bf16[2,128,256]{2,1,0:T(8,128)(2,1)S(1)}, bf16[2,128,256]{2,1,0:T(8,128)(2,1)S(1)}, bf16[2,128,256]{2,1,0:T(8,128)(2,1)S(1)}, bf16[2,128,256]{2...) custom-call(s32[8]{0:T(128)} %counts.11, ...), custom_call_target="tpu_custom_call" | custom-call | tf_op jit(solution)/shard_map/pallas_call | solution.py:485
  3.3 2.6 %collective-permute-start.16 = (bf16[2,128,256]{2,1,0:T(8,128)(2,1)S(1)}, bf16[2,128,256]{2,1,0:T(8,128)(2,1)S(1)}, u32[]{:S(2)}, u32[]{:S(2)}) collective-permute-start(bf16[2,128,256]{2,1,0:T(8,128)(2,1)S(1)} %get-tuple-element.49), channel_id=1, source_target_pairs={{0,8},{4,12},{8,0},{12,4},{16,24},{20,28},{24,16},{28,20},{1,9},{5... | collective-permute-start | bytes 393224 | tf_op jit(solution)/shard_map/ppermute | solution.py:521
  5.9 1.8 collective-permute-start.18
  7.7 4.0 %shard_map.91 = (bf16[2,128,640]{2,1,0:T(8,128)(2,1)S(1)}, bf16[2,128,640]{2,1,0:T(8,128)(2,1)}, bf16[2,128,640]{2,1,0:T(8,128)(2,1)S(1)}, bf16[2,128,640]{2,1,0...) custom-call(s32[8]{0:T(128)} %counts.11, ...), custom_call_target="tpu_custom_call" | custom-call | tf_op jit(solution)/shard_map/pallas_call | solution.py:485
  12.1 1.7 collective-permute-start.1
  13.9 1.5 collective-permute-start.20
  17.1 9.6 %collective-permute-done.20.refs_6_ = bf16[2,128,256]{2,1,0:T(8,128)(2,1)S(1)} collective-permute-done((bf16[2,128,256]{2,1,0:T(8,128)(2,1)S(1)}, bf16[2,128,256]{2,1,0:T(8,128)(2,1)S(1)}, u32[]{:S(2)}, u32[]{:S(2)}) %collective-permute-start.20) | collective-permute-done | bytes 131104 | tf_op jit(solution)/shard_map/ppermute | solution.py:521
  26.8 2.7 %shard_map.93 = bf16[8,2,136,128]{3,2,1,0:T(8,128)(2,1)} custom-call(s32[8]{0:T(128)} %counts.11, s32[8]{0:T(128)} %dest_order.11, s32[16,128]{1,0:T(8,128)} %refs_0_.4, bf16[2048,1024]{1,0:T(8,128)(2,1)} %refs_0_.5), custom_call_target="tpu_custom_call" | custom-call | tf_op jit(solution)/shard_map/pallas_call | solution.py:485
  29.5 4.0 %all-to-all-start = ((bf16[8,2,136,128]{3,2,1,0:T(8,128)(2,1)}), bf16[8,2,136,128]{3,2,1,0:T(8,128)(2,1)S(1)}, u32[]{:S(2)}, u32[]{:S(2)}) async-start(bf16[8,2,136,128]{3,2,1,0:T(8,128)(2,1)} %shard_map.93), calls=%async_computation | async-start | bytes 1114112 | tf_op jit(solution)/shard_map/all_to_all | solution.py:516
  33.4 1.4 collective-permute-done.21.refs_7_
  36.3 2.4 %collective-permute-start.5 = (bf16[2,128,640]{2,1,0:T(8,128)(2,1)}, bf16[2,128,640]{2,1,0:T(8,128)(2,1)S(1)}, u32[]{:S(2)}, u32[]{:S(2)}) collective-permute-start(bf16[2,128,640]{2,1,0:T(8,128)(2,1)} %get-tuple-element.43), channel_id=1, source_target_pairs={{0,24},{4,28},{8,16},{12,20},{16,8},{20,12},{24,0},{28,4},{1,25},{... | collective-permute-start | bytes 983048 | tf_op jit(solution)/shard_map/ppermute | solution.py:521
  38.8 1.0 copy-done.9
  41.6 1.3 shard_map.96.refs_6_
  43.6 1.6 collective-permute-start.22
  46.7 17.3 %collective-permute-done.4.refs_5_ = bf16[2,128,640]{2,1,0:T(8,128)(2,1)S(1)} collective-permute-done((bf16[2,128,640]{2,1,0:T(8,128)(2,1)}, bf16[2,128,640]{2,1,0:T(8,128)(2,1)S(1)}, u32[]{:S(2)}, u32[]{:S(2)}) %collective-permute-start.4) | collective-permute-done | bytes 327712 | tf_op jit(solution)/shard_map/ppermute | solution.py:521
  64.9 1.0 copy-done.3
  65.9 1.0 copy-done.5
  66.9 1.0 copy-done.7
  67.9 2.0 shard_map.92
  70.5 4.4 %collective-permute-start.7 = (bf16[256,640]{1,0:T(8,128)(2,1)}, bf16[256,640]{1,0:T(8,128)(2,1)}, u32[]{:S(2)}, u32[]{:S(2)}) collective-permute-start(bf16[256,640]{1,0:T(8,128)(2,1)} %get-tuple-element.45.refs_12_), channel_id=1, source_target_pairs={{0,1},{1,0},{2,3},{3,2},{4,5},{5,4},{6,7},{7,6},{8,9},{9,8},{10,11... | collective-permute-start | bytes 983048 | tf_op jit(solution)/shard_map/ppermute | solution.py:454
  76.6 3.7 %collective-permute-start.34 = (bf16[384,640]{1,0:T(8,128)(2,1)S(1)}, bf16[384,640]{1,0:T(8,128)(2,1)S(1)}, u32[]{:S(2)}, u32[]{:S(2)}) collective-permute-start(bf16[384,640]{1,0:T(8,128)(2,1)S(1)} %get-tuple-element.66.refs_12_), channel_id=1, source_target_pairs={{0,1},{1,0},{2,3},{3,2},{4,5},{5,4},{6,7},{7,6},{8,9},{9,8},{10,11... | collective-permute-start | bytes 1474568 | tf_op jit(solution)/shard_map/ppermute | solution.py:454
  81.0 2.8 %collective-permute-done.7.refs_13_ = bf16[256,640]{1,0:T(8,128)(2,1)} collective-permute-done((bf16[256,640]{1,0:T(8,128)(2,1)}, bf16[256,640]{1,0:T(8,128)(2,1)}, u32[]{:S(2)}, u32[]{:S(2)}) %collective-permute-start.7) | collective-permute-done | bytes 327712 | tf_op jit(solution)/shard_map/ppermute | solution.py:454
  84.5 4.8 %collective-permute-done.10.refs_1_ = bf16[1024,128]{1,0:T(8,128)(2,1)S(1)} collective-permute-done((bf16[1024,128]{1,0:T(8,128)(2,1)S(1)}, bf16[1024,128]{1,0:T(8,128)(2,1)S(1)}, u32[]{:S(2)}, u32[]{:S(2)}) %collective-permute-start.10) | collective-permute-done | bytes 262176 | tf_op jit(solution)/shard_map/ppermute | solution.py:454
  89.3 2.0 collective-permute-start.29
  92.1 1.3 collective-permute-start.24
  93.4 6.5 %collective-permute-done.34.refs_13_ = bf16[384,640]{1,0:T(8,128)(2,1)S(1)} collective-permute-done((bf16[384,640]{1,0:T(8,128)(2,1)S(1)}, bf16[384,640]{1,0:T(8,128)(2,1)S(1)}, u32[]{:S(2)}, u32[]{:S(2)}) %collective-permute-start.34) | collective-permute-done | bytes 491552 | tf_op jit(solution)/shard_map/ppermute | solution.py:454
  101.2 9.2 %collective-permute-done.29.refs_13_ = bf16[384,640]{1,0:T(8,128)(2,1)S(1)} collective-permute-done((bf16[384,640]{1,0:T(8,128)(2,1)S(1)}, bf16[384,640]{1,0:T(8,128)(2,1)S(1)}, u32[]{:S(2)}, u32[]{:S(2)}) %collective-permute-start.29) | collective-permute-done | bytes 491552 | tf_op jit(solution)/shard_map/ppermute | solution.py:454
  110.4 1.3 collective-permute-start.12
  111.7 1.3 collective-permute-start.26
  113.0 1.3 collective-permute-start.38
  115.0 12.2 %collective-permute-done.12.refs_3_ = bf16[1024,128]{1,0:T(8,128)(2,1)S(1)} collective-permute-done((bf16[1024,128]{1,0:T(8,128)(2,1)S(1)}, bf16[1024,128]{1,0:T(8,128)(2,1)S(1)}, u32[]{:S(2)}, u32[]{:S(2)}) %collective-permute-start.12) | collective-permute-done | bytes 262176 | tf_op jit(solution)/shard_map/ppermute | solution.py:454
  128.0 1.3 collective-permute-start.14
  129.3 24.5 %collective-permute-done.14.refs_5_ = bf16[1024,128]{1,0:T(8,128)(2,1)S(1)} collective-permute-done((bf16[1024,128]{1,0:T(8,128)(2,1)S(1)}, bf16[1024,128]{1,0:T(8,128)(2,1)S(1)}, u32[]{:S(2)}, u32[]{:S(2)}) %collective-permute-start.14) | collective-permute-done | bytes 262176 | tf_op jit(solution)/shard_map/ppermute | solution.py:454
  153.8 1.3 collective-permute-start.33
  155.1 4.6 %fetch.1 = (bf16[4096,1024]{1,0:T(8,128)(2,1)S(1)}, bf16[4096,512]{1,0:T(8,128)(2,1)S(1)}) custom-call(bf16[4096,1024]{1,0:T(8,128)(2,1)} %q_weight.1, bf16[4096,512]{1,0:T(8,128)(2,1)} %kv_weight.1), custom_call_target="tpu_custom_call" | custom-call | tf_op jit(solution)/shard_map/fetch/pallas_call | solution.py:504
  159.8 1.2 tables.1
  161.0 1.3 collective-permute-start.28
  162.3 1.3 collective-permute-start.9
  163.6 1.3 collective-permute-start.36
  164.9 1.3 collective-permute-start.31
  166.2 5.6 %shard_map.99 = (f32[384,1536]{1,0:T(8,128)S(1)}, f32[384,128]{1,0:T(8,128)S(1)}) custom-call(bf16[1024,128]{1,0:T(8,128)(2,1)S(1)} %get-tuple-element.46.refs_0_, bf16[1024,128]{1,0:T(8,128)(2,1)S(1)} %collective-permute-done.10.refs_1_, bf16[1024,128]{1,0:T(8,128)(2,1)S(1)} %collective-permute-done.11.refs_2_, ...), custom_call_target="tpu_custom_call" | custom-call | flops 4831838208 | bytes 16777216 | tf_op jit(solution)/shard_map/pallas_call | solution.py:575
  171.9 5.4 %shard_map.98 = (f32[384,1536]{1,0:T(8,128)S(1)}, f32[384,128]{1,0:T(8,128)S(1)}) custom-call(bf16[1024,128]{1,0:T(8,128)(2,1)S(1)} %get-tuple-element.46.refs_0_, bf16[1024,128]{1,0:T(8,128)(2,1)S(1)} %collective-permute-done.10.refs_1_, bf16[1024,128]{1,0:T(8,128)(2,1)S(1)} %collective-permute-done.11.refs_2_, ...), custom_call_target="tpu_custom_call" | custom-call | flops 4831838208 | bytes 16777216 | tf_op jit(solution)/shard_map/pallas_call | solution.py:575
  177.3 4.7 %shard_map.97 = (f32[256,1536]{1,0:T(8,128)S(1)}, f32[256,128]{1,0:T(8,128)S(1)}) custom-call(bf16[1024,128]{1,0:T(8,128)(2,1)S(1)} %get-tuple-element.46.refs_0_, bf16[1024,128]{1,0:T(8,128)(2,1)S(1)} %collective-permute-done.10.refs_1_, bf16[1024,128]{1,0:T(8,128)(2,1)S(1)} %collective-permute-done.11.refs_2_, ...), custom_call_target="tpu_custom_call" | custom-call | flops 3221225472 | bytes 16777216 | tf_op jit(solution)/shard_map/pallas_call | solution.py:575
  182.1 12.3 %collective-permute-done.36.refs_1_ = bf16[384,640]{1,0:T(8,128)(2,1)S(1)} collective-permute-done((bf16[384,640]{1,0:T(8,128)(2,1)S(1)}, bf16[384,640]{1,0:T(8,128)(2,1)S(1)}, u32[]{:S(2)}, u32[]{:S(2)}) %collective-permute-start.36) | collective-permute-done | bytes 491552 | tf_op jit(solution)/shard_map/ppermute | solution.py:454
  194.4 3.5 %shard_map.100.refs_10_ = bf16[1024,1024]{1,0:T(8,128)(2,1)} custom-call(bf16[384,640]{1,0:T(8,128)(2,1)S(1)} %collective-permute-done.35.refs_0_, bf16[384,640]{1,0:T(8,128)(2,1)S(1)} %collective-permute-done.36.refs_1_, f32[384,1536]{1,0:T(8,128)S(1)} %get-tuple-element.67.refs_2_, f32[384,128]{1,0:T(8,128)S(1)} %get-tuple-element.68.refs_3_, ...), custom_call_target="tpu_custom_call" | custom-call | flops 1207959552 | bytes 4194304 | tf_op jit(solution)/shard_map/pallas_call | solution.py:595
  197.8 5.3 %collective-permute-done.31.refs_1_ = bf16[384,640]{1,0:T(8,128)(2,1)S(1)} collective-permute-done((bf16[384,640]{1,0:T(8,128)(2,1)S(1)}, bf16[384,640]{1,0:T(8,128)(2,1)S(1)}, u32[]{:S(2)}, u32[]{:S(2)}) %collective-permute-start.31) | collective-permute-done | bytes 491552 | tf_op jit(solution)/shard_map/ppermute | solution.py:454
  203.2 3.3 %shard_map.101.refs_10_ = bf16[1024,1024]{1,0:T(8,128)(2,1)} custom-call(bf16[384,640]{1,0:T(8,128)(2,1)S(1)} %collective-permute-done.30.refs_0_, bf16[384,640]{1,0:T(8,128)(2,1)S(1)} %collective-permute-done.31.refs_1_, f32[384,1536]{1,0:T(8,128)S(1)} %get-tuple-element.64.refs_2_, ...), custom_call_target="tpu_custom_call", output_to_operand_aliasing={{}: (10, {})} | custom-call | flops 1207959552 | bytes 4194304 | tf_op jit(solution)/shard_map/pallas_call | solution.py:595
  206.5 2.6 %shard_map.102 = bf16[1024,1024]{1,0:T(8,128)(2,1)} custom-call(bf16[256,640]{1,0:T(8,128)(2,1)S(1)} %collective-permute-done.8.refs_0_, bf16[256,640]{1,0:T(8,128)(2,1)S(1)} %collective-permute-done.9.refs_1_, f32[256,1536]{1,0:T(8,128)S(1)} %get-tuple-element.57.refs_2_, ...), custom_call_target="tpu_custom_call", output_to_operand_aliasing={{}: (10, {})} | custom-call | flops 805306368 | bytes 4194304 | tf_op jit(solution)/shard_map/pallas_call | solution.py:595
  (81 shorter events, 16.4 us)
Async XLA Ops:
  2.8 8.9 %collective-permute-start.15 = (bf16[2,128,256]{2,1,0:T(8,128)(2,1)S(1)}, bf16[2,128,256]{2,1,0:T(8,128)(2,1)S(1)}, u32[]{:S(2)}, u32[]{:S(2)}) collective-permute-start(bf16[2,128,256]{2,1,0:T(8,128)(2,1)S(1)} %get-tuple-element.48), channel_id=1, source_target_pairs={{0,4},{4,0},{8,12},{12,8},{16,20},{20,16},{24,28},{28,24},{1,5},{5... | collective-permute-start | bytes 393224 | tf_op jit(solution)/shard_map/ppermute | solution.py:521
  3.3 8.8 %collective-permute-start.16 = (bf16[2,128,256]{2,1,0:T(8,128)(2,1)S(1)}, bf16[2,128,256]{2,1,0:T(8,128)(2,1)S(1)}, u32[]{:S(2)}, u32[]{:S(2)}) collective-permute-start(bf16[2,128,256]{2,1,0:T(8,128)(2,1)S(1)} %get-tuple-element.49), channel_id=1, source_target_pairs={{0,8},{4,12},{8,0},{12,4},{16,24},{20,28},{24,16},{28,20},{1,9},{5... | collective-permute-start | bytes 393224 | tf_op jit(solution)/shard_map/ppermute | solution.py:521
  5.9 8.0 %collective-permute-start.17 = (bf16[2,128,256]{2,1,0:T(8,128)(2,1)S(1)}, bf16[2,128,256]{2,1,0:T(8,128)(2,1)S(1)}, u32[]{:S(2)}, u32[]{:S(2)}) collective-permute-start(bf16[2,128,256]{2,1,0:T(8,128)(2,1)S(1)} %get-tuple-element.50), channel_id=1, source_target_pairs={{0,12},{4,8},{8,4},{12,0},{16,28},{20,24},{24,20},{28,16},{1,13},{... | collective-permute-start | bytes 393224 | tf_op jit(solution)/shard_map/ppermute | solution.py:521
  5.9 9.4 %collective-permute-start.18 = (bf16[2,128,256]{2,1,0:T(8,128)(2,1)S(1)}, bf16[2,128,256]{2,1,0:T(8,128)(2,1)S(1)}, u32[]{:S(2)}, u32[]{:S(2)}) collective-permute-start(bf16[2,128,256]{2,1,0:T(8,128)(2,1)S(1)} %get-tuple-element.51), channel_id=1, source_target_pairs={{0,16},{4,20},{8,24},{12,28},{16,0},{20,4},{24,8},{28,12},{1,17},{... | collective-permute-start | bytes 393224 | tf_op jit(solution)/shard_map/ppermute | solution.py:521
  7.7 8.3 %collective-permute-start.19 = (bf16[2,128,256]{2,1,0:T(8,128)(2,1)S(1)}, bf16[2,128,256]{2,1,0:T(8,128)(2,1)S(1)}, u32[]{:S(2)}, u32[]{:S(2)}) collective-permute-start(bf16[2,128,256]{2,1,0:T(8,128)(2,1)S(1)} %get-tuple-element.52), channel_id=1, source_target_pairs={{0,20},{4,16},{8,28},{12,24},{16,4},{20,0},{24,12},{28,8},{1,21},{... | collective-permute-start | bytes 393224 | tf_op jit(solution)/shard_map/ppermute | solution.py:521
  11.7 24.6 %collective-permute-start = (bf16[2,128,640]{2,1,0:T(8,128)(2,1)}, bf16[2,128,640]{2,1,0:T(8,128)(2,1)S(1)}, u32[]{:S(2)}, u32[]{:S(2)}) collective-permute-start(bf16[2,128,640]{2,1,0:T(8,128)(2,1)} %get-tuple-element.38), channel_id=1, source_target_pairs={{0,4},{4,0},{8,12},{12,8},{16,20},{20,16},{24,28},{28,24},{1,5},{5... | collective-permute-start | bytes 983048 | tf_op jit(solution)/shard_map/ppermute | solution.py:521
  12.1 26.6 %collective-permute-start.1 = (bf16[2,128,640]{2,1,0:T(8,128)(2,1)S(1)}, bf16[2,128,640]{2,1,0:T(8,128)(2,1)S(1)}, u32[]{:S(2)}, u32[]{:S(2)}) collective-permute-start(bf16[2,128,640]{2,1,0:T(8,128)(2,1)S(1)} %get-tuple-element.39), channel_id=1, source_target_pairs={{0,8},{4,12},{8,0},{12,4},{16,24},{20,28},{24,16},{28,20},{1,9},{5... | collective-permute-start | bytes 983048 | tf_op jit(solution)/shard_map/ppermute | solution.py:521
  13.9 12.9 %collective-permute-start.20 = (bf16[2,128,256]{2,1,0:T(8,128)(2,1)S(1)}, bf16[2,128,256]{2,1,0:T(8,128)(2,1)S(1)}, u32[]{:S(2)}, u32[]{:S(2)}) collective-permute-start(bf16[2,128,256]{2,1,0:T(8,128)(2,1)S(1)} %get-tuple-element.53), channel_id=1, source_target_pairs={{0,24},{4,28},{8,16},{12,20},{16,8},{20,12},{24,0},{28,4},{1,25},{... | collective-permute-start | bytes 393224 | tf_op jit(solution)/shard_map/ppermute | solution.py:521
  15.4 27.5 %collective-permute-start.2 = (bf16[2,128,640]{2,1,0:T(8,128)(2,1)}, bf16[2,128,640]{2,1,0:T(8,128)(2,1)S(1)}, u32[]{:S(2)}, u32[]{:S(2)}) collective-permute-start(bf16[2,128,640]{2,1,0:T(8,128)(2,1)} %get-tuple-element.40), channel_id=1, source_target_pairs={{0,12},{4,8},{8,4},{12,0},{16,28},{20,24},{24,20},{28,16},{1,13},{... | collective-permute-start | bytes 983048 | tf_op jit(solution)/shard_map/ppermute | solution.py:521
  16.6 28.6 %collective-permute-start.3 = (bf16[2,128,640]{2,1,0:T(8,128)(2,1)}, bf16[2,128,640]{2,1,0:T(8,128)(2,1)S(1)}, u32[]{:S(2)}, u32[]{:S(2)}) collective-permute-start(bf16[2,128,640]{2,1,0:T(8,128)(2,1)} %get-tuple-element.41), channel_id=1, source_target_pairs={{0,16},{4,20},{8,24},{12,28},{16,0},{20,4},{24,8},{28,12},{1,17},{... | collective-permute-start | bytes 983048 | tf_op jit(solution)/shard_map/ppermute | solution.py:521
  26.8 2.7 %copy-start.10 = (bf16[2,128,256]{2,1,0:T(8,128)(2,1)}, bf16[2,128,256]{2,1,0:T(8,128)(2,1)S(1)}, u32[]{:S(2)}) copy-start(bf16[2,128,256]{2,1,0:T(8,128)(2,1)S(1)} %collective-permute-done.20.refs_6_) | copy-start | bytes 393220
  26.8 8.1 %collective-permute-start.21 = (bf16[2,128,256]{2,1,0:T(8,128)(2,1)}, bf16[2,128,256]{2,1,0:T(8,128)(2,1)S(1)}, u32[]{:S(2)}, u32[]{:S(2)}) collective-permute-start(bf16[2,128,256]{2,1,0:T(8,128)(2,1)} %get-tuple-element.54), channel_id=1, source_target_pairs={{0,28},{4,24},{8,20},{12,16},{16,12},{20,8},{24,4},{28,0},{1,29},{... | collective-permute-start | bytes 393224 | tf_op jit(solution)/shard_map/ppermute | solution.py:521
  29.5 45.5 %all-to-all-start = ((bf16[8,2,136,128]{3,2,1,0:T(8,128)(2,1)}), bf16[8,2,136,128]{3,2,1,0:T(8,128)(2,1)S(1)}, u32[]{:S(2)}, u32[]{:S(2)}) async-start(bf16[8,2,136,128]{3,2,1,0:T(8,128)(2,1)} %shard_map.93), calls=%async_computation | async-start | bytes 1114112 | tf_op jit(solution)/shard_map/all_to_all | solution.py:516
  35.5 28.5 %collective-permute-start.4 = (bf16[2,128,640]{2,1,0:T(8,128)(2,1)}, bf16[2,128,640]{2,1,0:T(8,128)(2,1)S(1)}, u32[]{:S(2)}, u32[]{:S(2)}) collective-permute-start(bf16[2,128,640]{2,1,0:T(8,128)(2,1)} %get-tuple-element.42), channel_id=1, source_target_pairs={{0,20},{4,16},{8,28},{12,24},{16,4},{20,0},{24,12},{28,8},{1,21},{... | collective-permute-start | bytes 983048 | tf_op jit(solution)/shard_map/ppermute | solution.py:521
  36.3 27.6 %copy-start = (bf16[2,128,640]{2,1,0:T(8,128)(2,1)}, bf16[2,128,640]{2,1,0:T(8,128)(2,1)S(1)}, u32[]{:S(2)}) copy-start(bf16[2,128,640]{2,1,0:T(8,128)(2,1)S(1)} %collective-permute-done.refs_1_) | copy-start | bytes 983044
  36.3 27.6 %collective-permute-start.5 = (bf16[2,128,640]{2,1,0:T(8,128)(2,1)}, bf16[2,128,640]{2,1,0:T(8,128)(2,1)S(1)}, u32[]{:S(2)}, u32[]{:S(2)}) collective-permute-start(bf16[2,128,640]{2,1,0:T(8,128)(2,1)} %get-tuple-element.43), channel_id=1, source_target_pairs={{0,24},{4,28},{8,16},{12,20},{16,8},{20,12},{24,0},{28,4},{1,25},{... | collective-permute-start | bytes 983048 | tf_op jit(solution)/shard_map/ppermute | solution.py:521
  38.7 25.2 %copy-start.2 = (bf16[2,128,640]{2,1,0:T(8,128)(2,1)}, bf16[2,128,640]{2,1,0:T(8,128)(2,1)S(1)}, u32[]{:S(2)}) copy-start(bf16[2,128,640]{2,1,0:T(8,128)(2,1)S(1)} %collective-permute-done.1.refs_2_) | copy-start | bytes 983044
  38.7 25.2 %collective-permute-start.6 = (bf16[2,128,640]{2,1,0:T(8,128)(2,1)}, bf16[2,128,640]{2,1,0:T(8,128)(2,1)S(1)}, u32[]{:S(2)}, u32[]{:S(2)}) collective-permute-start(bf16[2,128,640]{2,1,0:T(8,128)(2,1)} %get-tuple-element.44), channel_id=1, source_target_pairs={{0,28},{4,24},{8,20},{12,16},{16,12},{20,8},{24,4},{28,0},{1,29},{... | collective-permute-start | bytes 983048 | tf_op jit(solution)/shard_map/ppermute | solution.py:521
  38.7 1.0 copy-start.9
  41.6 113.5 %copy-start.16 = (bf16[4096]{0:T(1024)(128)(2,1)S(1)}, bf16[4096]{0:T(1024)(128)(2,1)}, u32[]{:S(2)}) copy-start(bf16[4096]{0:T(1024)(128)(2,1)} %param.13) | copy-start | bytes 24580
  43.6 32.2 %collective-permute-start.22 = (bf16[1024,256]{1,0:T(8,128)(2,1)S(1)}, bf16[1024,256]{1,0:T(8,128)(2,1)S(1)}, u32[]{:S(2)}, u32[]{:S(2)}) collective-permute-start(bf16[1024,256]{1,0:T(8,128)(2,1)S(1)} %shard_map.96.refs_6_), channel_id=1, source_target_pairs={{0,1},{1,0},{2,3},{3,2},{4,5},{5,4},{6,7},{7,6},{8,9},{9,8},{10,11... | collective-permute-start | bytes 1572872 | tf_op jit(solution)/shard_map/ppermute | solution.py:454
  46.0 30.6 %collective-permute-start.23 = (bf16[1024,256]{1,0:T(8,128)(2,1)S(1)}, bf16[1024,256]{1,0:T(8,128)(2,1)S(1)}, u32[]{:S(2)}, u32[]{:S(2)}) collective-permute-start(bf16[1024,256]{1,0:T(8,128)(2,1)S(1)} %shard_map.96.refs_6_), channel_id=1, source_target_pairs={{1,2},{2,1},{5,6},{6,5},{9,10},{10,9},{13,14},{14,13},{17,18},{18,... | collective-permute-start | bytes 1572872 | tf_op jit(solution)/shard_map/ppermute | solution.py:454
  64.0 1.0 copy-start.1
  69.8 10.5 %collective-permute-start.27 = (bf16[256,640]{1,0:T(8,128)(2,1)}, bf16[256,640]{1,0:T(8,128)(2,1)S(1)}, u32[]{:S(2)}, u32[]{:S(2)}) collective-permute-start(bf16[256,640]{1,0:T(8,128)(2,1)} %get-tuple-element.45.refs_12_), channel_id=1, source_target_pairs={{1,2},{2,1},{5,6},{6,5},{9,10},{10,9},{13,14},{14,13},{17,18},{18,... | collective-permute-start | bytes 983048 | tf_op jit(solution)/shard_map/ppermute | solution.py:454
  70.5 13.3 %collective-permute-start.7 = (bf16[256,640]{1,0:T(8,128)(2,1)}, bf16[256,640]{1,0:T(8,128)(2,1)}, u32[]{:S(2)}, u32[]{:S(2)}) collective-permute-start(bf16[256,640]{1,0:T(8,128)(2,1)} %get-tuple-element.45.refs_12_), channel_id=1, source_target_pairs={{0,1},{1,0},{2,3},{3,2},{4,5},{5,4},{6,7},{7,6},{8,9},{9,8},{10,11... | collective-permute-start | bytes 983048 | tf_op jit(solution)/shard_map/ppermute | solution.py:454
  75.8 13.6 %collective-permute-start.10 = (bf16[1024,128]{1,0:T(8,128)(2,1)S(1)}, bf16[1024,128]{1,0:T(8,128)(2,1)S(1)}, u32[]{:S(2)}, u32[]{:S(2)}) collective-permute-start(bf16[1024,128]{1,0:T(8,128)(2,1)S(1)} %get-tuple-element.46.refs_0_), channel_id=1, source_target_pairs={{0,1},{1,0},{2,3},{3,2},{4,5},{5,4},{6,7},{7,6},{8,9},{9,8},{10,11... | collective-permute-start | bytes 786440 | tf_op jit(solution)/shard_map/ppermute | solution.py:454
  75.9 16.2 %collective-permute-start.37 = (bf16[384,640]{1,0:T(8,128)(2,1)S(1)}, bf16[384,640]{1,0:T(8,128)(2,1)S(1)}, u32[]{:S(2)}, u32[]{:S(2)}) collective-permute-start(bf16[384,640]{1,0:T(8,128)(2,1)S(1)} %get-tuple-element.66.refs_12_), channel_id=1, source_target_pairs={{1,2},{2,1},{5,6},{6,5},{9,10},{10,9},{13,14},{14,13},{17,18},{18,... | collective-permute-start | bytes 1474568 | tf_op jit(solution)/shard_map/ppermute | solution.py:454
  76.6 23.3 %collective-permute-start.34 = (bf16[384,640]{1,0:T(8,128)(2,1)S(1)}, bf16[384,640]{1,0:T(8,128)(2,1)S(1)}, u32[]{:S(2)}, u32[]{:S(2)}) collective-permute-start(bf16[384,640]{1,0:T(8,128)(2,1)S(1)} %get-tuple-element.66.refs_12_), channel_id=1, source_target_pairs={{0,1},{1,0},{2,3},{3,2},{4,5},{5,4},{6,7},{7,6},{8,9},{9,8},{10,11... | collective-permute-start | bytes 1474568 | tf_op jit(solution)/shard_map/ppermute | solution.py:454
  80.3 11.0 %collective-permute-start.11 = (bf16[1024,128]{1,0:T(8,128)(2,1)S(1)}, bf16[1024,128]{1,0:T(8,128)(2,1)S(1)}, u32[]{:S(2)}, u32[]{:S(2)}) collective-permute-start(bf16[1024,128]{1,0:T(8,128)(2,1)S(1)} %get-tuple-element.46.refs_0_), channel_id=1, source_target_pairs={{1,2},{2,1},{5,6},{6,5},{9,10},{10,9},{13,14},{14,13},{17,18},{18,... | collective-permute-start | bytes 786440 | tf_op jit(solution)/shard_map/ppermute | solution.py:454
  83.8 16.7 %collective-permute-start.32 = (bf16[384,640]{1,0:T(8,128)(2,1)S(1)}, bf16[384,640]{1,0:T(8,128)(2,1)S(1)}, u32[]{:S(2)}, u32[]{:S(2)}) collective-permute-start(bf16[384,640]{1,0:T(8,128)(2,1)S(1)} %get-tuple-element.63.refs_12_), channel_id=1, source_target_pairs={{1,2},{2,1},{5,6},{6,5},{9,10},{10,9},{13,14},{14,13},{17,18},{18,... | collective-permute-start | bytes 1474568 | tf_op jit(solution)/shard_map/ppermute | solution.py:454
  89.3 21.1 %collective-permute-start.29 = (bf16[384,640]{1,0:T(8,128)(2,1)S(1)}, bf16[384,640]{1,0:T(8,128)(2,1)S(1)}, u32[]{:S(2)}, u32[]{:S(2)}) collective-permute-start(bf16[384,640]{1,0:T(8,128)(2,1)S(1)} %get-tuple-element.63.refs_12_), channel_id=1, source_target_pairs={{0,1},{1,0},{2,3},{3,2},{4,5},{5,4},{6,7},{7,6},{8,9},{9,8},{10,11... | collective-permute-start | bytes 1474568 | tf_op jit(solution)/shard_map/ppermute | solution.py:454
  91.4 20.3 %collective-permute-start.25 = (bf16[1024,256]{1,0:T(8,128)(2,1)S(1)}, bf16[1024,256]{1,0:T(8,128)(2,1)S(1)}, u32[]{:S(2)}, u32[]{:S(2)}) collective-permute-start(bf16[1024,256]{1,0:T(8,128)(2,1)S(1)} %collective-permute-done.22.refs_7_), channel_id=1, source_target_pairs={{1,2},{2,1},{5,6},{6,5},{9,10},{10,9},{13,14},{14,13},{17,18},{18,... | collective-permute-start | bytes 1572872 | tf_op jit(solution)/shard_map/ppermute | solution.py:454
  92.1 35.9 %collective-permute-start.24 = (bf16[1024,256]{1,0:T(8,128)(2,1)S(1)}, bf16[1024,256]{1,0:T(8,128)(2,1)S(1)}, u32[]{:S(2)}, u32[]{:S(2)}) collective-permute-start(bf16[1024,256]{1,0:T(8,128)(2,1)S(1)} %collective-permute-done.23.refs_8_), channel_id=1, source_target_pairs={{1,0},{2,3},{5,4},{6,7},{9,8},{10,11},{13,12},{14,15},{17,16},{18,... | collective-permute-start | bytes 1572872 | tf_op jit(solution)/shard_map/ppermute | solution.py:454
  99.9 13.1 %collective-permute-start.8 = (bf16[256,640]{1,0:T(8,128)(2,1)}, bf16[256,640]{1,0:T(8,128)(2,1)S(1)}, u32[]{:S(2)}, u32[]{:S(2)}) collective-permute-start(bf16[256,640]{1,0:T(8,128)(2,1)} %collective-permute-done.7.refs_13_), channel_id=1, source_target_pairs={{1,2},{2,1},{5,6},{6,5},{9,10},{10,9},{13,14},{14,13},{17,18},{18,... | collective-permute-start | bytes 983048 | tf_op jit(solution)/shard_map/ppermute | solution.py:454
  100.6 13.8 %collective-permute-start.13 = (bf16[1024,128]{1,0:T(8,128)(2,1)S(1)}, bf16[1024,128]{1,0:T(8,128)(2,1)S(1)}, u32[]{:S(2)}, u32[]{:S(2)}) collective-permute-start(bf16[1024,128]{1,0:T(8,128)(2,1)S(1)} %collective-permute-done.10.refs_1_), channel_id=1, source_target_pairs={{1,2},{2,1},{5,6},{6,5},{9,10},{10,9},{13,14},{14,13},{17,18},{18,... | collective-permute-start | bytes 786440 | tf_op jit(solution)/shard_map/ppermute | solution.py:454
  110.4 16.9 %collective-permute-start.12 = (bf16[1024,128]{1,0:T(8,128)(2,1)S(1)}, bf16[1024,128]{1,0:T(8,128)(2,1)S(1)}, u32[]{:S(2)}, u32[]{:S(2)}) collective-permute-start(bf16[1024,128]{1,0:T(8,128)(2,1)S(1)} %collective-permute-done.11.refs_2_), channel_id=1, source_target_pairs={{1,0},{2,3},{5,4},{6,7},{9,8},{10,11},{13,12},{14,15},{17,16},{18,... | collective-permute-start | bytes 786440 | tf_op jit(solution)/shard_map/ppermute | solution.py:454
  111.7 53.2 %collective-permute-start.26 = (bf16[1024,256]{1,0:T(8,128)(2,1)S(1)}, bf16[1024,256]{1,0:T(8,128)(2,1)S(1)}, u32[]{:S(2)}, u32[]{:S(2)}) collective-permute-start(bf16[1024,256]{1,0:T(8,128)(2,1)S(1)} %collective-permute-done.25.refs_10_), channel_id=1, source_target_pairs={{1,0},{2,3},{5,4},{6,7},{9,8},{10,11},{13,12},{14,15},{17,16},{18,... | collective-permute-start | bytes 1572872 | tf_op jit(solution)/shard_map/ppermute | solution.py:454
  113.0 48.0 %collective-permute-start.38 = (bf16[384,640]{1,0:T(8,128)(2,1)S(1)}, bf16[384,640]{1,0:T(8,128)(2,1)S(1)}, u32[]{:S(2)}, u32[]{:S(2)}) collective-permute-start(bf16[384,640]{1,0:T(8,128)(2,1)S(1)} %collective-permute-done.37.refs_14_), channel_id=1, source_target_pairs={{1,0},{2,3},{5,4},{6,7},{9,8},{10,11},{13,12},{14,15},{17,16},{18,... | collective-permute-start | bytes 1474568 | tf_op jit(solution)/shard_map/ppermute | solution.py:454
  114.3 48.0 %collective-permute-start.35 = (bf16[384,640]{1,0:T(8,128)(2,1)S(1)}, bf16[384,640]{1,0:T(8,128)(2,1)S(1)}, u32[]{:S(2)}, u32[]{:S(2)}) collective-permute-start(bf16[384,640]{1,0:T(8,128)(2,1)S(1)} %collective-permute-done.34.refs_13_), channel_id=1, source_target_pairs={{1,2},{2,1},{5,6},{6,5},{9,10},{10,9},{13,14},{14,13},{17,18},{18,... | collective-permute-start | bytes 1474568 | tf_op jit(solution)/shard_map/ppermute | solution.py:454
  127.3 36.4 %collective-permute-start.30 = (bf16[384,640]{1,0:T(8,128)(2,1)S(1)}, bf16[384,640]{1,0:T(8,128)(2,1)S(1)}, u32[]{:S(2)}, u32[]{:S(2)}) collective-permute-start(bf16[384,640]{1,0:T(8,128)(2,1)S(1)} %collective-permute-done.29.refs_13_), channel_id=1, source_target_pairs={{1,2},{2,1},{5,6},{6,5},{9,10},{10,9},{13,14},{14,13},{17,18},{18,... | collective-permute-start | bytes 1474568 | tf_op jit(solution)/shard_map/ppermute | solution.py:454
  128.0 25.8 %collective-permute-start.14 = (bf16[1024,128]{1,0:T(8,128)(2,1)S(1)}, bf16[1024,128]{1,0:T(8,128)(2,1)S(1)}, u32[]{:S(2)}, u32[]{:S(2)}) collective-permute-start(bf16[1024,128]{1,0:T(8,128)(2,1)S(1)} %collective-permute-done.13.refs_4_), channel_id=1, source_target_pairs={{1,0},{2,3},{5,4},{6,7},{9,8},{10,11},{13,12},{14,15},{17,16},{18,... | collective-permute-start | bytes 786440 | tf_op jit(solution)/shard_map/ppermute | solution.py:454
  153.8 18.1 %collective-permute-start.33 = (bf16[384,640]{1,0:T(8,128)(2,1)S(1)}, bf16[384,640]{1,0:T(8,128)(2,1)S(1)}, u32[]{:S(2)}, u32[]{:S(2)}) collective-permute-start(bf16[384,640]{1,0:T(8,128)(2,1)S(1)} %collective-permute-done.32.refs_14_), channel_id=1, source_target_pairs={{1,0},{2,3},{5,4},{6,7},{9,8},{10,11},{13,12},{14,15},{17,16},{18,... | collective-permute-start | bytes 1474568 | tf_op jit(solution)/shard_map/ppermute | solution.py:454
  155.1 4.7 %copy-start.14 = (f32[128,128]{1,0:T(8,128)S(1)}, f32[128,128]{1,0:T(8,128)}, u32[]{:S(2)}) copy-start(f32[128,128]{1,0:T(8,128)} %constant.4.clone.cosines) | copy-start | bytes 196612
  155.1 4.7 %copy-start.15 = (f32[128,128]{1,0:T(8,128)S(1)}, f32[128,128]{1,0:T(8,128)}, u32[]{:S(2)}) copy-start(f32[128,128]{1,0:T(8,128)} %constant.5.clone.sines) | copy-start | bytes 196612
  161.0 16.3 %collective-permute-start.28 = (bf16[256,640]{1,0:T(8,128)(2,1)S(1)}, bf16[256,640]{1,0:T(8,128)(2,1)S(1)}, u32[]{:S(2)}, u32[]{:S(2)}) collective-permute-start(bf16[256,640]{1,0:T(8,128)(2,1)S(1)} %collective-permute-done.27.refs_14_), channel_id=1, source_target_pairs={{1,0},{2,3},{5,4},{6,7},{9,8},{10,11},{13,12},{14,15},{17,16},{18,... | collective-permute-start | bytes 983048 | tf_op jit(solution)/shard_map/ppermute | solution.py:454
  162.3 44.1 %collective-permute-start.9 = (bf16[256,640]{1,0:T(8,128)(2,1)S(1)}, bf16[256,640]{1,0:T(8,128)(2,1)S(1)}, u32[]{:S(2)}, u32[]{:S(2)}) collective-permute-start(bf16[256,640]{1,0:T(8,128)(2,1)S(1)} %collective-permute-done.8.refs_0_), channel_id=1, source_target_pairs={{1,0},{2,3},{5,4},{6,7},{9,8},{10,11},{13,12},{14,15},{17,16},{18,... | collective-permute-start | bytes 983048 | tf_op jit(solution)/shard_map/ppermute | solution.py:454
  163.6 30.7 %collective-permute-start.36 = (bf16[384,640]{1,0:T(8,128)(2,1)S(1)}, bf16[384,640]{1,0:T(8,128)(2,1)S(1)}, u32[]{:S(2)}, u32[]{:S(2)}) collective-permute-start(bf16[384,640]{1,0:T(8,128)(2,1)S(1)} %collective-permute-done.35.refs_0_), channel_id=1, source_target_pairs={{1,0},{2,3},{5,4},{6,7},{9,8},{10,11},{13,12},{14,15},{17,16},{18,... | collective-permute-start | bytes 1474568 | tf_op jit(solution)/shard_map/ppermute | solution.py:454
  164.9 38.2 %collective-permute-start.31 = (bf16[384,640]{1,0:T(8,128)(2,1)S(1)}, bf16[384,640]{1,0:T(8,128)(2,1)S(1)}, u32[]{:S(2)}, u32[]{:S(2)}) collective-permute-start(bf16[384,640]{1,0:T(8,128)(2,1)S(1)} %collective-permute-done.30.refs_0_), channel_id=1, source_target_pairs={{1,0},{2,3},{5,4},{6,7},{9,8},{10,11},{13,12},{14,15},{17,16},{18,... | collective-permute-start | bytes 1474568 | tf_op jit(solution)/shard_map/ppermute | solution.py:454
  (9 other events, 7.5 us)
